TPU v7x, 64 devices: a 2x2x8 block of a 4x4x8 slice. The times are simulated.
64 devices in a mesh: dp: 4 (over x, y), cp: 16 (over z, core).
Axes of the slice: x: 2, y: 2, z: 8, core: 2. Of those that a mesh axis runs over, the one named last changes fastest.
The devices are a block of a 4x4x8 slice.
Arguments:
- hidden: bfloat16 [64, 1024, 1152], P('dp', 'cp'), parts along dimension 0
- positions: int32 [64, 1024], P('dp', 'cp'), parts along dimension 0
- wq_local: bfloat16 [1152, 1024], replicated
- wk_local: bfloat16 [1152, 256], replicated
- wv_local: bfloat16 [1152, 256], replicated
- wo_local: bfloat16 [1024, 1152], replicated
- wgate_local: bfloat16 [1152, 6912], replicated
- wup_local: bfloat16 [1152, 6912], replicated
- wdown_local: bfloat16 [6912, 1152], replicated
- preatt_local: float32 [1152], replicated
- postatt_local: float32 [1152], replicated
- preffw_local: float32 [1152], replicated
- postffw_local: float32 [1152], replicated
- wq_global: bfloat16 [1152, 1024], replicated
- wk_global: bfloat16 [1152, 256], replicated
- wv_global: bfloat16 [1152, 256], replicated
- wo_global: bfloat16 [1024, 1152], replicated
- wgate_global: bfloat16 [1152, 6912], replicated
- wup_global: bfloat16 [1152, 6912], replicated
- wdown_global: bfloat16 [6912, 1152], replicated
- preatt_global: float32 [1152], replicated
- postatt_global: float32 [1152], replicated
- preffw_global: float32 [1152], replicated
- postffw_global: float32 [1152], replicated
Outputs:
- output: bfloat16 [64, 1024, 1152], P('dp', 'cp'), parts along dimension 0
There are 4 independent parts. A program takes and returns all parts, laid end to end along the dimension named above; an argument that names none is the same for every part.
All inputs are finite; a program needn't handle non-finite values.
Results may differ from a plain program's by a relative error of at most 0.02.
Values are sent between devices in bfloat16 or wider.
A program may use at most 768 MiB of HBM per device.

v0:
```python
import jax
import jax.numpy as jnp
from jax import lax
from jax.sharding import PartitionSpec as P

HEAD_DIM = 256
WINDOW = 512
EPSILON = 1e-6
THETA = 10000.0
SOFT_CAP = 50.0


def rms_norm(inputs, norm_scale):
    widened = inputs.astype(jnp.float32)
    mean_sq = jnp.mean(widened * widened, axis=-1, keepdims=True)
    return (widened * lax.rsqrt(mean_sq + EPSILON) * (1.0 + norm_scale)).astype(jnp.bfloat16)


def rope_tables(tok_pos):
    half_dim = HEAD_DIM // 2
    inv_freq = THETA ** (-(jnp.arange(half_dim, dtype=jnp.float32) * 2.0 / HEAD_DIM))
    angles = tok_pos.astype(jnp.float32)[:, :, None, None] * inv_freq
    return jnp.cos(angles), jnp.sin(angles)


def apply_rope(heads_in, cos_t, sin_t):
    half_dim = HEAD_DIM // 2
    widened = heads_in.astype(jnp.float32)
    first_half = widened[..., :half_dim]
    second_half = widened[..., half_dim:]
    return jnp.concatenate([first_half * cos_t - second_half * sin_t, second_half * cos_t + first_half * sin_t], axis=-1)


def project_qkv(hidden, cos_t, sin_t, weights):
    w_q, w_k, w_v, pre_att = weights[0], weights[1], weights[2], weights[7]
    batch_rows, tok_len = hidden.shape[0], hidden.shape[1]
    kv_heads = w_k.shape[1] // HEAD_DIM
    group_size = w_q.shape[1] // w_k.shape[1]
    normed = rms_norm(hidden, pre_att)
    q_raw = jnp.einsum("btd,dn->btn", normed, w_q, preferred_element_type=jnp.float32).astype(jnp.bfloat16)
    k_raw = jnp.einsum("btd,dn->btn", normed, w_k, preferred_element_type=jnp.float32).astype(jnp.bfloat16)
    v_raw = jnp.einsum("btd,dn->btn", normed, w_v, preferred_element_type=jnp.float32).astype(jnp.bfloat16)
    query_rot = apply_rope(q_raw.reshape(batch_rows, tok_len, kv_heads * group_size, HEAD_DIM), cos_t, sin_t)
    query_rot = (query_rot * HEAD_DIM ** -0.5).astype(jnp.bfloat16).reshape(batch_rows, tok_len, kv_heads, group_size, HEAD_DIM)
    key_rot = apply_rope(k_raw.reshape(batch_rows, tok_len, kv_heads, HEAD_DIM), cos_t, sin_t).astype(jnp.bfloat16)
    value_t = v_raw.reshape(batch_rows, tok_len, kv_heads, HEAD_DIM)
    return query_rot, key_rot, value_t


def attend(query_rot, key_all, value_all, q_pos, k_pos, window_len):
    scores = jnp.einsum("btkgd,bskd->bkgts", query_rot, key_all, preferred_element_type=jnp.float32)
    capped = SOFT_CAP * jnp.tanh(scores / SOFT_CAP)
    offset = q_pos[:, None, None, :, None] - k_pos[:, None, None, None, :]
    visible = (offset >= 0) & (offset < window_len)
    prob_bf = jax.nn.softmax(jnp.where(visible, capped, -1e30), axis=-1).astype(jnp.bfloat16)
    mixed_heads = jnp.einsum("bkgts,bskd->btkgd", prob_bf, value_all, preferred_element_type=jnp.float32).astype(jnp.bfloat16)
    return mixed_heads.reshape(query_rot.shape[0], query_rot.shape[1], -1)


def finish_layer(hidden, mixed_heads, weights):
    w_o, w_gate, w_up, w_down = weights[3], weights[4], weights[5], weights[6]
    post_att, pre_ffw, post_ffw = weights[8], weights[9], weights[10]
    attn_out = jnp.einsum("btn,nd->btd", mixed_heads, w_o, preferred_element_type=jnp.float32).astype(jnp.bfloat16)
    mid_state = (hidden.astype(jnp.float32) + rms_norm(attn_out, post_att).astype(jnp.float32)).astype(jnp.bfloat16)
    normed_mid = rms_norm(mid_state, pre_ffw)
    gate_val = jnp.einsum("btd,df->btf", normed_mid, w_gate, preferred_element_type=jnp.float32).astype(jnp.bfloat16)
    up_val = jnp.einsum("btd,df->btf", normed_mid, w_up, preferred_element_type=jnp.float32).astype(jnp.bfloat16)
    act_val = (jax.nn.gelu(gate_val.astype(jnp.float32), approximate=True) * up_val.astype(jnp.float32)).astype(jnp.bfloat16)
    down_val = jnp.einsum("btf,fd->btd", act_val, w_down, preferred_element_type=jnp.float32).astype(jnp.bfloat16)
    return (mid_state.astype(jnp.float32) + rms_norm(down_val, post_ffw).astype(jnp.float32)).astype(jnp.bfloat16)


def solution(mesh):
    cp_size = mesh.shape["cp"]

    def device_step(hidden, positions, *weights):
        local_w = weights[:11]
        global_w = weights[11:]
        chunk_len = hidden.shape[1]
        my_index = lax.axis_index("cp")
        all_pos = lax.all_gather(positions, "cp", axis=1, tiled=True)
        cos_t, sin_t = rope_tables(positions)
        n_prev = (WINDOW + chunk_len - 2) // chunk_len
        query_rot, key_rot, value_t = project_qkv(hidden, cos_t, sin_t, local_w)
        key_parts = [key_rot]
        value_parts = [value_t]
        pos_parts = [positions]
        for shift_by in range(1, n_prev + 1):
            perm_pairs = [(source_idx, source_idx + shift_by) for source_idx in range(cp_size - shift_by)]
            key_parts.append(lax.ppermute(key_rot, "cp", perm_pairs))
            value_parts.append(lax.ppermute(value_t, "cp", perm_pairs))
            start_at = ((my_index - shift_by) % cp_size) * chunk_len
            pos_parts.append(lax.dynamic_slice_in_dim(all_pos, start_at, chunk_len, axis=1))
        mixed_heads = attend(query_rot, jnp.concatenate(key_parts, axis=1), jnp.concatenate(value_parts, axis=1), positions, jnp.concatenate(pos_parts, axis=1), WINDOW)
        mid_hidden = finish_layer(hidden, mixed_heads, local_w)
        query_rot, key_rot, value_t = project_qkv(mid_hidden, cos_t, sin_t, global_w)
        key_all = lax.all_gather(key_rot, "cp", axis=1, tiled=True)
        value_all = lax.all_gather(value_t, "cp", axis=1, tiled=True)
        mixed_heads = attend(query_rot, key_all, value_all, positions, all_pos, 2 * chunk_len * cp_size)
        return finish_layer(mid_hidden, mixed_heads, global_w)

    specs_in = tuple([P("dp", "cp"), P("dp", "cp")] + [P()] * 22)
    return jax.shard_map(device_step, mesh=mesh, in_specs=specs_in, out_specs=P("dp", "cp"), check_vma=False)
```

profile of v0, /device:TPU:21, one launch (start us, length us, event | category | flops | bytes accessed | tf_op | source)
XLA Modules:
  0.0 732.7 jit_solution(2430021405615089540)
XLA Ops:
  7.4 2.2 fusion.68
  10.4 2.7 fusion.135
  13.1 2.3 fusion.157
  16.5 5.1 collective-permute-start.8
  21.6 4.6 collective-permute-start.9
  26.2 3.7 collective-permute-start.10
  30.0 5.7 collective-permute-start.11
  35.7 3.8 collective-permute-start.12
  39.5 1.9 multiply_cosine_fusion
  42.1 71.5 %all-gather.1 = s32[16,64,16]{1,2,0:T(8,128)S(1)} all-gather(s32[1,64,16]{1,2,0:T(8,128)S(1)} %bitcast.192), channel_id=1, replica_groups=mesh['dp'=4,'cp'=16] {'cp'}, dimensions={0}, use_global_device_ids=true | all-gather | bytes 69632 | tf_op jit(solution)/shard_map/all_gather | solution.py:81
  116.8 1.5 fusion.104
  118.4 7.4 %convert_convert_fusion.1 = f32[16,64,1024]{2,1,0:T(8,128)} fusion(bf16[1152,1024]{1,0:T(8,128)(2,1)} %param.26, bf16[16,64,1152]{2,1,0:T(8,128)(2,1)} %param.24, f32[1152]{0:T(1024)} %copy-done.24, f32[16,64]{1,0:T(8,128)} %copy-done.26), kind=kOutput, calls=%fused_computation.140 | convolution fusion | flops 2422734848 | bytes 8921600 | tf_op jit(solution)/shard_map/btd,dn->btn/dot_general | solution.py:40
  125.7 5.7 reshape.287
  131.4 2.8 fusion.183
  134.5 1.9 constant_dynamic-update-slice_fusion.8
  136.4 2.8 multiply_subtract_fusion.1
  139.9 10.1 %collective-permute-start.13 = (bf16[16,64,1,256]{3,1,0,2:T(8,128)(2,1)}, bf16[16,64,1,256]{3,1,0,2:T(8,128)(2,1)S(1)}, u32[]{:S(2)}, u32[]{:S(2)}) collective-permute-start(bf16[16,64,1,256]{3,1,0,2:T(8,128)(2,1)} %get-tuple-element.23), channel_id=1, source_target_pairs={{0,6},{1,7},{2,8},{3,9},{4,10},{5,11},{6,12},{7,13},{8,14},{9,15},... | collective-permute-start | bytes 1572872 | tf_op jit(solution)/shard_map/ppermute | solution.py:90
  151.2 4.6 collective-permute-start.14
  156.9 1.3 collective-permute-start.15
  159.4 2.4 collective-permute-start
  162.9 2.1 collective-permute-start.1
  166.1 52.5 %collective-permute-start.2 = (bf16[16,64,1,256]{3,1,0,2:T(8,128)(2,1)}, bf16[16,64,1,256]{3,1,0,2:T(8,128)(2,1)}, u32[]{:S(2)}, u32[]{:S(2)}) collective-permute-start(bf16[16,64,1,256]{3,1,0,2:T(8,128)(2,1)} %get-tuple-element.38), channel_id=1, source_target_pairs={{0,3},{1,4},{2,5},{3,6},{4,7},{5,8},{6,9},{7,10},{8,11},{9,12},{10... | collective-permute-start | bytes 1572872 | tf_op jit(solution)/shard_map/ppermute | solution.py:91
  218.7 10.0 %collective-permute-start.3 = (bf16[16,64,1,256]{3,1,0,2:T(8,128)(2,1)}, bf16[16,64,1,256]{3,1,0,2:T(8,128)(2,1)}, u32[]{:S(2)}, u32[]{:S(2)}) collective-permute-start(bf16[16,64,1,256]{3,1,0,2:T(8,128)(2,1)} %get-tuple-element.38), channel_id=1, source_target_pairs={{0,4},{1,5},{2,6},{3,7},{4,8},{5,9},{6,10},{7,11},{8,12},{9,13},{1... | collective-permute-start | bytes 1572872 | tf_op jit(solution)/shard_map/ppermute | solution.py:91
  228.8 25.2 %collective-permute-start.4 = (bf16[16,64,1,256]{3,1,0,2:T(8,128)(2,1)}, bf16[16,64,1,256]{3,1,0,2:T(8,128)(2,1)}, u32[]{:S(2)}, u32[]{:S(2)}) collective-permute-start(bf16[16,64,1,256]{3,1,0,2:T(8,128)(2,1)} %get-tuple-element.38), channel_id=1, source_target_pairs={{0,5},{1,6},{2,7},{3,8},{4,9},{5,10},{6,11},{7,12},{8,13},{9,14},{... | collective-permute-start | bytes 1572872 | tf_op jit(solution)/shard_map/ppermute | solution.py:91
  254.1 2.1 copy-done.14
  256.2 6.9 fusion.52
  263.1 4.8 fusion.47
  267.9 1.3 collective-permute-start.5
  269.3 1.9 constant_dynamic-update-slice_fusion.7
  271.2 6.1 collective-permute-start.6
  277.3 1.9 constant_dynamic-update-slice_fusion.6
  279.1 1.7 collective-permute-start.7
  280.8 1.9 constant_dynamic-update-slice_fusion.5
  282.7 1.9 constant_dynamic-update-slice_fusion.4
  284.6 1.9 constant_dynamic-update-slice_fusion.3
  288.4 5.0 collective-permute-done.7
  294.2 6.7 convert_bitcast_fusion.1
  300.9 4.7 copy.44
  305.6 4.4 reshape.280
  310.1 4.7 fusion.56
  314.8 1.3 fusion.72
  316.1 24.4 %fusion.24 = bf16[16,64,6912]{2,1,0:T(8,128)(2,1)} fusion(bf16[1152,6912]{1,0:T(8,128)(2,1)} %param.30, bf16[16,64,1152]{2,1,0:T(8,128)(2,1)S(1)} %get-tuple-element.10, f32[1152]{0:T(1024)S(1)} %broadcast_add_fusion.5, f32[16,64]{1,0:T(8,128)S(1)} %add_rsqrt_fusion.5), kind=kOutput, calls=%fused_computation.35 | convolution fusion | flops 16312172544 | bytes 32449024 | tf_op jit(solution)/shard_map/btd,df->btf/dot_general | solution.py:66
  340.5 28.2 %fusion.96.clone.4 = bf16[16,64,6912]{2,1,0:T(8,128)(2,1)} fusion(bf16[1152,6912]{1,0:T(8,128)(2,1)} %param.31, bf16[16,64,6912]{2,1,0:T(8,128)(2,1)} %fusion.24, bf16[16,64,1152]{2,1,0:T(8,128)(2,1)S(1)} %get-tuple-element.10, f32[1152]{0:T(1024)S(1)} %broadcast_add_fusion.5, f32[16,64]{1,0:T(8,128)S(1)} %add_rsqrt_fusion.5), kind=kOutput, calls=%fused_computation.14.clone.clone.clone.clone.clone.clone.1 | convolution fusion | flops 16404185088 | bytes 46604800 | tf_op jit(solution)/shard_map/btd,df->btf/dot_general | solution.py:67
  368.7 23.4 %fusion.59 = (f32[16,64]{1,0:T(8,128)S(1)}, bf16[16,64,1152]{2,1,0:T(8,128)(2,1)S(1)}) fusion(bf16[6912,1152]{1,0:T(8,128)(2,1)} %param.32, bf16[16,64,6912]{2,1,0:T(8,128)(2,1)} %fusion.96.clone.4), kind=kOutput, calls=%fused_computation.85 | convolution fusion | flops 16312171520 | bytes 32444416 | tf_op jit(solution)/shard_map/btf,fd->btd/dot_general | solution.py:69
  392.2 1.4 fusion.76
  394.6 2.3 fusion.161
  398.0 1.7 convolution_convert_fusion.3
  401.4 6.5 convert_convert_fusion
  407.9 5.7 reshape.289
  413.6 2.7 fusion.182
  416.3 2.8 multiply_subtract_fusion
  419.2 151.0 %all-gather.5.cloned.1.call-done = bf16[16,1024,1,256]{3,1,0,2:T(8,128)(2,1)} async-done(((bf16[16,64,1,256]{3,1,0,2:T(8,128)(2,1)}), bf16[16,1024,1,256]{3,1,0,2:T(8,128)(2,1)}) %all-gather.5.cloned.1.call-update) | async-done | bytes 8388624 | tf_op jit(solution)/shard_map/all_gather | solution.py:97
  570.2 11.5 %fusion.188 = (f32[16,4,64]{2,1,0:T(4,128)S(1)}, f32[16,1,4,64,1024]{4,3,2,0,1:T(8,128)}) fusion(f32[16,64,4,128]{3,1,2,0:T(8,128)} %get-tuple-element.12, f32[16,64,4,128]{3,1,2,0:T(8,128)} %get-tuple-element.11, bf16[16,1024,1,256]{3,1,0,2:T(8,128)(2,1)} %all-gather.5.cloned.1.call-done, pred[16,64,1024]{2,1,0:T(8,128)(4,1)S(1)} %fusion.89), kind=kOutput, calls=%fused_computation.236 | convolution fusion | flops 2167402496 | bytes 30425088 | tf_op jit(solution)/shard_map/btkgd,bskd->bkgts/dot_general | solution.py:51
  581.7 7.4 %fusion.26 = f32[16,4,64]{2,1,0:T(4,128)S(1)} fusion(f32[16,1,4,64,1024]{4,3,2,0,1:T(8,128)} %get-tuple-element.44, f32[16,4,64]{2,1,0:T(4,128)S(1)} %get-tuple-element.43), kind=kLoop, calls=%fused_computation.37 | loop fusion | flops 8384512 | bytes 16809984 | tf_op jit(solution)/shard_map/reduce_sum | solution.py:55
  589.1 33.8 %all-gather.7.cloned.1.call-done = bf16[16,1024,256]{2,1,0:T(8,128)(2,1)} async-done(((bf16[16,64,256]{2,1,0:T(8,128)(2,1)}), bf16[16,1024,256]{2,1,0:T(8,128)(2,1)}) %all-gather.7.cloned.1.call-update) | async-done | bytes 8388624 | tf_op jit(solution)/shard_map/all_gather | solution.py:98
  622.9 9.9 %convert_bitcast_fusion = bf16[16,64,1,4,256]{4,1,3,0,2:T(8,128)(2,1)S(1)} fusion(f32[16,4,64]{2,1,0:T(4,128)S(1)} %fusion.26, f32[16,1,4,64,1024]{4,3,2,0,1:T(8,128)} %get-tuple-element.44, f32[16,4,64]{2,1,0:T(4,128)S(1)} %get-tuple-element.43, bf16[16,1024,256]{2,1,0:T(8,128)(2,1)} %all-gather.7.cloned.1.call-done), kind=kOutput, calls=%fused_computation.131 | convolution fusion | flops 2161115136 | bytes 27295744 | tf_op jit(solution)/shard_map/bkgts,bskd->btkgd/dot_general | solution.py:56
  632.8 3.1 copy.47
  635.8 4.9 reshape.285
  640.7 5.2 fusion.62
  646.0 1.4 fusion.80
  647.3 24.2 %fusion.18 = bf16[16,64,6912]{2,1,0:T(8,128)(2,1)} fusion(bf16[1152,6912]{1,0:T(8,128)(2,1)} %param.41, bf16[16,64,1152]{2,1,0:T(8,128)(2,1)S(1)} %get-tuple-element.6, f32[1152]{0:T(1024)S(1)} %broadcast_add_fusion.1, f32[16,64]{1,0:T(8,128)S(1)} %add_rsqrt_fusion.1), kind=kOutput, calls=%fused_computation.29 | convolution fusion | flops 16312172544 | bytes 32449024 | tf_op jit(solution)/shard_map/btd,df->btf/dot_general | solution.py:66
  671.6 28.3 %fusion.103.clone.2 = bf16[16,64,6912]{2,1,0:T(8,128)(2,1)} fusion(bf16[1152,6912]{1,0:T(8,128)(2,1)} %param.42, bf16[16,64,6912]{2,1,0:T(8,128)(2,1)} %fusion.18, bf16[16,64,1152]{2,1,0:T(8,128)(2,1)S(1)} %get-tuple-element.6, f32[1152]{0:T(1024)S(1)} %broadcast_add_fusion.1, f32[16,64]{1,0:T(8,128)S(1)} %add_rsqrt_fusion.1), kind=kOutput, calls=%fused_computation.21.clone.clone.clone.clone.clone.clone | convolution fusion | flops 16404185088 | bytes 46604800 | tf_op jit(solution)/shard_map/btd,df->btf/dot_general | solution.py:67
  699.9 23.3 %fusion.65 = (f32[16,64]{1,0:T(8,128)S(1)}, bf16[16,64,1152]{2,1,0:T(8,128)(2,1)S(1)}) fusion(bf16[6912,1152]{1,0:T(8,128)(2,1)} %param.43, bf16[16,64,6912]{2,1,0:T(8,128)(2,1)} %fusion.103.clone.2), kind=kOutput, calls=%fused_computation.91 | convolution fusion | flops 16312171520 | bytes 32444416 | tf_op jit(solution)/shard_map/btf,fd->btd/dot_general | solution.py:69
  723.3 2.4 fusion.83
  (128 shorter events, 19.5 us)
Async XLA Ops:
  6.5 303.5 %copy-start = (bf16[1024,1152]{1,0:T(8,128)(2,1)S(1)}, bf16[1024,1152]{1,0:T(8,128)(2,1)}, u32[]{:S(2)}) copy-start(bf16[1024,1152]{1,0:T(8,128)(2,1)} %param.29) | copy-start | bytes 7077892
  6.6 563.6 %all-gather.5.cloned.1.call-start = ((), (), s32[]{:S(2)}) async-start(), calls=%async_computation | async-start | bytes 8912896 | tf_op jit(solution)/shard_map/all_gather | solution.py:97
  6.6 32.9 %copy-start.29 = (f32[128]{0:T(128)}, f32[128]{0:T(128)S(1)}, u32[]{:S(2)}) copy-start(f32[128]{0:T(128)S(1)} %negate_power_fusion) | copy-start | bytes 1540
  7.4 8.0 %copy-start.24 = (f32[1152]{0:T(1024)}, f32[1152]{0:T(1024)S(1)}, u32[]{:S(2)}) copy-start(f32[1152]{0:T(1024)S(1)} %broadcast_add_fusion.7) | copy-start | bytes 13828
  9.6 29.8 %copy-start.26 = (f32[16,64]{1,0:T(8,128)}, f32[16,64]{1,0:T(8,128)S(1)}, u32[]{:S(2)}) copy-start(f32[16,64]{1,0:T(8,128)S(1)} %add_rsqrt_fusion.7) | copy-start | bytes 12292
  10.3 29.1 %copy-start.12 = (f32[16,64]{1,0:T(8,128)}, f32[16,64]{1,0:T(8,128)S(1)}, u32[]{:S(2)}) copy-start(f32[16,64]{1,0:T(8,128)S(1)} %convert_element_type.221) | copy-start | bytes 12292
  10.3 31.0 %copy-start.17 = (f32[1152]{0:T(1024)S(1)}, f32[1152]{0:T(1024)}, u32[]{:S(2)}) copy-start(f32[1152]{0:T(1024)} %param.36) | copy-start | bytes 13828
  10.4 31.7 %copy-start.10 = (s32[16,64]{1,0:T(8,128)S(1)}, s32[16,64]{1,0:T(8,128)}, u32[]{:S(2)}) copy-start(s32[16,64]{1,0:T(8,128)} %param.25) | copy-start | bytes 12292
  16.5 123.4 %collective-permute-start.8 = (bf16[16,64,1,256]{3,1,0,2:T(8,128)(2,1)}, bf16[16,64,1,256]{3,1,0,2:T(8,128)(2,1)}, u32[]{:S(2)}, u32[]{:S(2)}) collective-permute-start(bf16[16,64,1,256]{3,1,0,2:T(8,128)(2,1)} %get-tuple-element.23), channel_id=1, source_target_pairs={{0,1},{1,2},{2,3},{3,4},{4,5},{5,6},{6,7},{7,8},{8,9},{9,10},{10,1... | collective-permute-start | bytes 1572872 | tf_op jit(solution)/shard_map/ppermute | solution.py:90
  21.6 129.5 %collective-permute-start.9 = (bf16[16,64,1,256]{3,1,0,2:T(8,128)(2,1)}, bf16[16,64,1,256]{3,1,0,2:T(8,128)(2,1)}, u32[]{:S(2)}, u32[]{:S(2)}) collective-permute-start(bf16[16,64,1,256]{3,1,0,2:T(8,128)(2,1)} %get-tuple-element.23), channel_id=1, source_target_pairs={{0,2},{1,3},{2,4},{3,5},{4,6},{5,7},{6,8},{7,9},{8,10},{9,11},{10,... | collective-permute-start | bytes 1572872 | tf_op jit(solution)/shard_map/ppermute | solution.py:90
  26.2 130.7 %collective-permute-start.10 = (bf16[16,64,1,256]{3,1,0,2:T(8,128)(2,1)}, bf16[16,64,1,256]{3,1,0,2:T(8,128)(2,1)}, u32[]{:S(2)}, u32[]{:S(2)}) collective-permute-start(bf16[16,64,1,256]{3,1,0,2:T(8,128)(2,1)} %get-tuple-element.23), channel_id=1, source_target_pairs={{0,3},{1,4},{2,5},{3,6},{4,7},{5,8},{6,9},{7,10},{8,11},{9,12},{10... | collective-permute-start | bytes 1572872 | tf_op jit(solution)/shard_map/ppermute | solution.py:90
  30.0 129.4 %collective-permute-start.11 = (bf16[16,64,1,256]{3,1,0,2:T(8,128)(2,1)}, bf16[16,64,1,256]{3,1,0,2:T(8,128)(2,1)}, u32[]{:S(2)}, u32[]{:S(2)}) collective-permute-start(bf16[16,64,1,256]{3,1,0,2:T(8,128)(2,1)} %get-tuple-element.23), channel_id=1, source_target_pairs={{0,4},{1,5},{2,6},{3,7},{4,8},{5,9},{6,10},{7,11},{8,12},{9,13},{1... | collective-permute-start | bytes 1572872 | tf_op jit(solution)/shard_map/ppermute | solution.py:90
  35.7 127.3 %collective-permute-start.12 = (bf16[16,64,1,256]{3,1,0,2:T(8,128)(2,1)}, bf16[16,64,1,256]{3,1,0,2:T(8,128)(2,1)}, u32[]{:S(2)}, u32[]{:S(2)}) collective-permute-start(bf16[16,64,1,256]{3,1,0,2:T(8,128)(2,1)} %get-tuple-element.23), channel_id=1, source_target_pairs={{0,5},{1,6},{2,7},{3,8},{4,9},{5,10},{6,11},{7,12},{8,13},{9,14},{... | collective-permute-start | bytes 1572872 | tf_op jit(solution)/shard_map/ppermute | solution.py:90
  41.4 95.0 %copy-start.4 = (f32[16,64,128]{2,1,0:T(8,128)}, f32[16,64,128]{2,1,0:T(8,128)S(1)}, u32[]{:S(2)}) copy-start(f32[16,64,128]{2,1,0:T(8,128)S(1)} %get-tuple-element.33) | copy-start | bytes 1572868
  41.4 95.0 %copy-start.6 = (f32[16,64,128]{2,1,0:T(8,128)}, f32[16,64,128]{2,1,0:T(8,128)S(1)}, u32[]{:S(2)}) copy-start(f32[16,64,128]{2,1,0:T(8,128)S(1)} %get-tuple-element.34) | copy-start | bytes 1572868
  115.2 10.5 %copy-start.8 = (s32[1024,16]{0,1:T(8,128)}, s32[1024,16]{0,1:T(8,128)S(1)}, u32[]{:S(2)}) copy-start(s32[1024,16]{0,1:T(8,128)S(1)} %reshape.293) | copy-start | bytes 196612
  131.4 2.9 copy-start.2
  131.4 2.9 copy-start.25
  131.4 2.9 copy-start.27
  131.4 3.1 copy-start.31
  134.5 15.6 %slice-start = ((s8[4718592]{0:T(1024)(128)(4,1)}), s8[4194304]{0:T(1024)(128)(4,1)S(1)}, s32[]{:S(2)}) async-start(s8[4718592]{0:T(1024)(128)(4,1)} %bitcast.193), calls=%async_computation.2 | async-start | bytes 8388608
  136.4 2.8 copy-start.18
  136.4 2.8 copy-start.19
  136.4 2.8 copy-start.20
  136.4 13.6 %slice-start.1 = ((s8[4718592]{0:T(1024)(128)(4,1)}), s8[524288]{0:T(1024)(128)(4,1)S(1)}, s32[]{:S(2)}) async-start(s8[4718592]{0:T(1024)(128)(4,1)} %bitcast.193), calls=%async_computation.3 | async-start | bytes 1048576
  139.9 26.2 %collective-permute-start.13 = (bf16[16,64,1,256]{3,1,0,2:T(8,128)(2,1)}, bf16[16,64,1,256]{3,1,0,2:T(8,128)(2,1)S(1)}, u32[]{:S(2)}, u32[]{:S(2)}) collective-permute-start(bf16[16,64,1,256]{3,1,0,2:T(8,128)(2,1)} %get-tuple-element.23), channel_id=1, source_target_pairs={{0,6},{1,7},{2,8},{3,9},{4,10},{5,11},{6,12},{7,13},{8,14},{9,15},... | collective-permute-start | bytes 1572872 | tf_op jit(solution)/shard_map/ppermute | solution.py:90
  151.2 67.5 %collective-permute-start.14 = (bf16[16,64,1,256]{3,1,0,2:T(8,128)(2,1)}, bf16[16,64,1,256]{3,1,0,2:T(8,128)(2,1)S(1)}, u32[]{:S(2)}, u32[]{:S(2)}) collective-permute-start(bf16[16,64,1,256]{3,1,0,2:T(8,128)(2,1)} %get-tuple-element.23), channel_id=1, source_target_pairs={{0,7},{1,8},{2,9},{3,10},{4,11},{5,12},{6,13},{7,14},{8,15},{16,23... | collective-permute-start | bytes 1572872 | tf_op jit(solution)/shard_map/ppermute | solution.py:90
  156.9 71.9 %collective-permute-start.15 = (bf16[16,64,1,256]{3,1,0,2:T(8,128)(2,1)}, bf16[16,64,1,256]{3,1,0,2:T(8,128)(2,1)S(1)}, u32[]{:S(2)}, u32[]{:S(2)}) collective-permute-start(bf16[16,64,1,256]{3,1,0,2:T(8,128)(2,1)} %get-tuple-element.23), channel_id=1, source_target_pairs={{0,8},{1,9},{2,10},{3,11},{4,12},{5,13},{6,14},{7,15},{16,24},{17,... | collective-permute-start | bytes 1572872 | tf_op jit(solution)/shard_map/ppermute | solution.py:90
  159.4 108.6 %collective-permute-start = (bf16[16,64,1,256]{3,1,0,2:T(8,128)(2,1)}, bf16[16,64,1,256]{3,1,0,2:T(8,128)(2,1)}, u32[]{:S(2)}, u32[]{:S(2)}) collective-permute-start(bf16[16,64,1,256]{3,1,0,2:T(8,128)(2,1)} %get-tuple-element.38), channel_id=1, source_target_pairs={{0,1},{1,2},{2,3},{3,4},{4,5},{5,6},{6,7},{7,8},{8,9},{9,10},{10,1... | collective-permute-start | bytes 1572872 | tf_op jit(solution)/shard_map/ppermute | solution.py:91
  162.9 108.3 %collective-permute-start.1 = (bf16[16,64,1,256]{3,1,0,2:T(8,128)(2,1)}, bf16[16,64,1,256]{3,1,0,2:T(8,128)(2,1)}, u32[]{:S(2)}, u32[]{:S(2)}) collective-permute-start(bf16[16,64,1,256]{3,1,0,2:T(8,128)(2,1)} %get-tuple-element.38), channel_id=1, source_target_pairs={{0,2},{1,3},{2,4},{3,5},{4,6},{5,7},{6,8},{7,9},{8,10},{9,11},{10,... | collective-permute-start | bytes 1572872 | tf_op jit(solution)/shard_map/ppermute | solution.py:91
  166.1 113.0 %collective-permute-start.2 = (bf16[16,64,1,256]{3,1,0,2:T(8,128)(2,1)}, bf16[16,64,1,256]{3,1,0,2:T(8,128)(2,1)}, u32[]{:S(2)}, u32[]{:S(2)}) collective-permute-start(bf16[16,64,1,256]{3,1,0,2:T(8,128)(2,1)} %get-tuple-element.38), channel_id=1, source_target_pairs={{0,3},{1,4},{2,5},{3,6},{4,7},{5,8},{6,9},{7,10},{8,11},{9,12},{10... | collective-permute-start | bytes 1572872 | tf_op jit(solution)/shard_map/ppermute | solution.py:91
  218.7 64.0 %collective-permute-start.3 = (bf16[16,64,1,256]{3,1,0,2:T(8,128)(2,1)}, bf16[16,64,1,256]{3,1,0,2:T(8,128)(2,1)}, u32[]{:S(2)}, u32[]{:S(2)}) collective-permute-start(bf16[16,64,1,256]{3,1,0,2:T(8,128)(2,1)} %get-tuple-element.38), channel_id=1, source_target_pairs={{0,4},{1,5},{2,6},{3,7},{4,8},{5,9},{6,10},{7,11},{8,12},{9,13},{1... | collective-permute-start | bytes 1572872 | tf_op jit(solution)/shard_map/ppermute | solution.py:91
  228.8 55.8 %collective-permute-start.4 = (bf16[16,64,1,256]{3,1,0,2:T(8,128)(2,1)}, bf16[16,64,1,256]{3,1,0,2:T(8,128)(2,1)}, u32[]{:S(2)}, u32[]{:S(2)}) collective-permute-start(bf16[16,64,1,256]{3,1,0,2:T(8,128)(2,1)} %get-tuple-element.38), channel_id=1, source_target_pairs={{0,5},{1,6},{2,7},{3,8},{4,9},{5,10},{6,11},{7,12},{8,13},{9,14},{... | collective-permute-start | bytes 1572872 | tf_op jit(solution)/shard_map/ppermute | solution.py:91
  254.1 2.1 copy-start.14
  267.9 18.5 %collective-permute-start.5 = (bf16[16,64,1,256]{3,1,0,2:T(8,128)(2,1)}, bf16[16,64,1,256]{3,1,0,2:T(8,128)(2,1)S(1)}, u32[]{:S(2)}, u32[]{:S(2)}) collective-permute-start(bf16[16,64,1,256]{3,1,0,2:T(8,128)(2,1)} %get-tuple-element.38), channel_id=1, source_target_pairs={{0,6},{1,7},{2,8},{3,9},{4,10},{5,11},{6,12},{7,13},{8,14},{9,15},... | collective-permute-start | bytes 1572872 | tf_op jit(solution)/shard_map/ppermute | solution.py:91
  271.2 16.3 %collective-permute-start.6 = (bf16[16,64,1,256]{3,1,0,2:T(8,128)(2,1)}, bf16[16,64,1,256]{3,1,0,2:T(8,128)(2,1)S(1)}, u32[]{:S(2)}, u32[]{:S(2)}) collective-permute-start(bf16[16,64,1,256]{3,1,0,2:T(8,128)(2,1)} %get-tuple-element.38), channel_id=1, source_target_pairs={{0,7},{1,8},{2,9},{3,10},{4,11},{5,12},{6,13},{7,14},{8,15},{16,23... | collective-permute-start | bytes 1572872 | tf_op jit(solution)/shard_map/ppermute | solution.py:91
  279.1 14.2 %collective-permute-start.7 = (bf16[16,64,1,256]{3,1,0,2:T(8,128)(2,1)}, bf16[16,64,1,256]{3,1,0,2:T(8,128)(2,1)S(1)}, u32[]{:S(2)}, u32[]{:S(2)}) collective-permute-start(bf16[16,64,1,256]{3,1,0,2:T(8,128)(2,1)} %get-tuple-element.38), channel_id=1, source_target_pairs={{0,8},{1,9},{2,10},{3,11},{4,12},{5,13},{6,14},{7,15},{16,24},{17,... | collective-permute-start | bytes 1572872 | tf_op jit(solution)/shard_map/ppermute | solution.py:91
  310.1 4.7 copy-start.3
  368.7 23.4 %copy-start.16 = (f32[1152]{0:T(1024)S(1)}, f32[1152]{0:T(1024)}, u32[]{:S(2)}) copy-start(f32[1152]{0:T(1024)} %broadcast_add_fusion.4) | copy-start | bytes 13828
  392.1 1.4 copy-start.28
  392.1 1.4 copy-start.32
  393.5 1.0 copy-start.13
  393.5 1.0 copy-start.30
  393.5 4.4 copy-start.33
  394.5 5.2 copy-start.21
  394.5 5.2 copy-start.22
  394.6 5.2 copy-start.23
  394.6 5.8 copy-start.9
  394.6 5.8 copy-start.11
  397.9 225.0 %all-gather.7.cloned.1.call-start = ((), (), s32[]{:S(2)}) async-start(), calls=%async_computation.1 | async-start | bytes 8912896 | tf_op jit(solution)/shard_map/all_gather | solution.py:98
  413.6 2.8 copy-start.5
  413.6 2.8 copy-start.7
  699.9 23.4 %copy-start.15 = (f32[1152]{0:T(1024)S(1)}, f32[1152]{0:T(1024)}, u32[]{:S(2)}) copy-start(f32[1152]{0:T(1024)} %broadcast_add_fusion) | copy-start | bytes 13828
  699.9 25.8 %copy-start.1 = (bf16[1024,1152]{1,0:T(8,128)(2,1)S(1)}, bf16[1024,1152]{1,0:T(8,128)(2,1)}, u32[]{:S(2)}) copy-start(bf16[1024,1152]{1,0:T(8,128)(2,1)} %param.29) | copy-start | bytes 7077892
Sparse Core Ops, SparseCore 0:
  398.0 172.1 all-gather.4
  571.8 51.0 all-gather.6
where the time goes:
time: 743 us; the launch traced here: 733 us
  matrix products  218 us (29%)
  waiting for transfers between devices  190 us (26%)
  starting transfers between devices  141 us (19%)
  blocking collectives  71.5 us (10%)
  local copies, waits for them, and re-layouts  57.2 us (8%)
  other arithmetic  41.1 us (6%)
  between operations  14.4 us (2%)
    all_gather x1, waiting for transfers between devices, device_step(): key_all = lax.all_gather(key_rot, 'cp', axis=1, tiled=True)  151 us
    ppermute x8, starting transfers between devices, device_step(): value_parts.append(lax.ppermute(value_t, 'cp', perm_pairs))  101 us
    all_gather x1, blocking collectives, device_step(): all_pos = lax.all_gather(positions, 'cp', axis=1, tiled=True)  71.5 us
    dot_general x2, matrix products, finish_layer(): jnp.einsum('btd,df->btf', normed_mid, w_up, preferred_element_type=jnp.fl...  56.5 us
    dot_general x2, matrix products, finish_layer(): jnp.einsum('btd,df->btf', normed_mid, w_gate, preferred_element_type=jnp....  48.6 us
    dot_general x2, matrix products, finish_layer(): jnp.einsum('btf,fd->btd', act_val, w_down, preferred_element_type=jnp.flo...  46.7 us
    ppermute x8, starting transfers between devices, device_step(): key_parts.append(lax.ppermute(key_rot, 'cp', perm_pairs))  39.1 us
    all_gather x1, waiting for transfers between devices, device_step(): value_all = lax.all_gather(value_t, 'cp', axis=1, tiled=True)  33.8 us
  transfers between devices with their start and end apart: 18, of which 4 were waited for; matrix products, arithmetic and copies ran while one was open for 13% of the time, Pallas kernels for 0%

commit v1 on v0

v1 whole, which is shorter than its diff:
```python
import functools

import jax
import jax.numpy as jnp
from jax import lax
from jax.experimental import pallas as pl
from jax.experimental.pallas import tpu as pltpu
from jax.sharding import PartitionSpec as P

HEAD_DIM = 256
HALF_DIM = HEAD_DIM // 2
WINDOW = 512
EPSILON = 1e-6
THETA = 10000.0
SOFT_CAP = 50.0
LOG2E = 1.4426950408889634
GELU_A = 0.7978845608028654
F_TILE = 768
RING = 4
BF16 = jnp.bfloat16
F32 = jnp.float32


def dot(lhs, rhs):
    return jnp.dot(lhs, rhs, preferred_element_type=F32)


def gelu_times(gate, up):
    gate = gate.astype(BF16).astype(F32)
    up = up.astype(BF16).astype(F32)
    inner = gate * (GELU_A + (GELU_A * 0.044715) * (gate * gate))
    scaled = (0.5 * gate) * up
    return (scaled + scaled * jnp.tanh(inner)).astype(BF16)


def rms(rows, scale):
    mean_sq = jnp.mean(rows * rows, axis=-1, keepdims=True)
    return (rows * lax.rsqrt(mean_sq + EPSILON) * scale).astype(BF16)


def rope(raw, cos_t, sin_t):
    raw = raw.astype(BF16).astype(F32)
    first, second = raw[:, :HALF_DIM], raw[:, HALF_DIM:]
    return first * cos_t - second * sin_t, second * cos_t + first * sin_t


def fused_kernel(cp_size, hidden, pos_rows, scales, inv_freq, *refs):
    weights = (refs[0:7], refs[7:14])
    out = refs[14]
    (xb, ab, qs, kb, vb, ob, oacc, lacc, posb, pcol, prow, cos_b, sin_b, acc, hb, w_qkv, w_o, w_g, w_u, w_d,
     w_sem, ring_sem, x_send, x_recv, p_send, p_recv, kv_send, kv_recv, o_send, o_recv) = refs[15:]
    n_chips = cp_size // 2
    piece = hidden.shape[1]
    dim = hidden.shape[2]
    slots = xb.shape[1] // piece
    quarter = slots // 2
    q_len = quarter * piece
    n_tok = xb.shape[1]
    n_heads = w_o.shape[1] // HEAD_DIM
    ffn = weights[0][4].shape[1]
    n_tiles = ffn // F_TILE
    me = lax.axis_index("cp")
    chip, core = me // 2, me % 2
    my_quarter = me // quarter
    my_core = jnp.where((my_quarter == 0) | (my_quarter == 3), 0, 1)
    my_slot = me % quarter + jnp.where(my_quarter >= 2, quarter, 0)

    def quarter_of(which_core, idx):
        return which_core + idx * (3 - 2 * which_core)

    w_copies = []
    for layer in range(2):
        wq, wk, wv, wo = weights[layer][:4]
        q_wide = wq.shape[1]
        w_copies += [
            pltpu.make_async_copy(wq, w_qkv.at[layer, :, pl.ds(0, q_wide)], w_sem.at[layer, 0]),
            pltpu.make_async_copy(wk, w_qkv.at[layer, :, pl.ds(q_wide, HEAD_DIM)], w_sem.at[layer, 1]),
            pltpu.make_async_copy(wv, w_qkv.at[layer, :, pl.ds(q_wide + HEAD_DIM, HEAD_DIM)], w_sem.at[layer, 2]),
            pltpu.make_async_copy(wo, w_o.at[layer], w_sem.at[layer, 3]),
        ]

    def tile_copies(layer, tile, buf):
        gate, up, down = weights[layer][4:7]
        cols = pl.ds(pl.multiple_of(tile * F_TILE, F_TILE), F_TILE)
        return (
            pltpu.make_async_copy(gate.at[:, cols], w_g.at[buf], ring_sem.at[0, buf]),
            pltpu.make_async_copy(up.at[:, cols], w_u.at[buf], ring_sem.at[1, buf]),
            pltpu.make_async_copy(down.at[cols, :], w_d.at[buf], ring_sem.at[2, buf]),
        )

    def start_tile(count):
        layer, tile, buf = (count // n_tiles) % 2, count % n_tiles, count % RING

        @pl.when(layer == 0)
        def _():
            for copy in tile_copies(0, tile, buf):
                copy.start()

        @pl.when(layer == 1)
        def _():
            for copy in tile_copies(1, tile, buf):
                copy.start()

    barrier = pltpu.get_barrier_semaphore()
    for shift in range(1, cp_size):
        pl.semaphore_signal(barrier, inc=1, device_id={"cp": lax.rem(me + shift, cp_size)}, device_id_type=pl.DeviceIdType.MESH)
    pl.semaphore_wait(barrier, cp_size - 1)

    order = sorted(range(1, n_chips), key=lambda d: -min(d, n_chips - d)) + [0]

    def x_copy(half, shift):
        to_chip = lax.rem(chip + shift, n_chips)
        return pltpu.make_async_remote_copy(
            src_ref=hidden.at[half * n_chips + to_chip], dst_ref=xb.at[half, pl.ds(my_slot * piece, piece), :],
            send_sem=x_send.at[half, shift], recv_sem=x_recv.at[half, my_slot],
            device_id={"cp": 2 * to_chip + my_core}, device_id_type=pl.DeviceIdType.MESH)

    def x_local(half):
        return pltpu.make_async_copy(hidden.at[half * n_chips + chip], xb.at[half, pl.ds(my_slot * piece, piece), :], x_recv.at[half, my_slot])

    def p_copy(shift, to_core):
        to_chip = lax.rem(chip + shift, n_chips)
        return pltpu.make_async_remote_copy(
            src_ref=pos_rows.at[to_chip], dst_ref=posb.at[me], send_sem=p_send.at[shift, to_core], recv_sem=p_recv.at[me],
            device_id={"cp": 2 * to_chip + to_core}, device_id_type=pl.DeviceIdType.MESH)

    def p_local():
        return pltpu.make_async_copy(pos_rows.at[chip], posb.at[me], p_recv.at[me])

    for shift in order:
        for to_core in range(2):
            if shift:
                p_copy(shift, to_core).start()
            else:
                @pl.when(core != to_core)
                def _():
                    p_copy(shift, to_core).start()
    p_local().start()
    for half in range(2):
        for shift in order:
            if shift:
                x_copy(half, shift).start()
            else:
                @pl.when(my_core != core)
                def _():
                    x_copy(half, shift).start()

                @pl.when(my_core == core)
                def _():
                    x_local(half).start()

    for copy in w_copies:
        copy.start()
    for count in range(RING - 1):
        start_tile(count)

    for from_piece in range(cp_size):
        pltpu.make_async_copy(pos_rows.at[0], posb.at[from_piece], p_recv.at[from_piece]).wait()
    for copy in w_copies:
        copy.wait()

    def kv_copy(slot, idx, which):
        buf = (kb, vb)[which]
        rows = pl.ds(pl.multiple_of(quarter_of(core, idx) * q_len, q_len), q_len)
        return pltpu.make_async_remote_copy(
            src_ref=buf.at[slot, rows, :], dst_ref=buf.at[slot, rows, :], send_sem=kv_send.at[slot, idx, which],
            recv_sem=kv_recv.at[slot, idx, which], device_id={"cp": 2 * chip + 1 - core}, device_id_type=pl.DeviceIdType.MESH)

    def o_copy(half, slot):
        idx = slot // quarter
        to_piece = quarter_of(core, idx) * quarter + slot % quarter
        return to_piece, pltpu.make_async_remote_copy(
            src_ref=xb.at[half, pl.ds(slot * piece, piece), :], dst_ref=out.at[half * n_chips + chip],
            send_sem=o_send.at[half, slot], recv_sem=o_recv.at[half, chip],
            device_id={"cp": to_piece}, device_id_type=pl.DeviceIdType.MESH)

    def stage(count, carry):
        half, layer = count // 2, count % 2
        kv_slot = count % 2

        @pl.when(layer == 0)
        def _():
            for slot in range(slots):
                pltpu.make_async_copy(hidden.at[0], xb.at[half, pl.ds(slot * piece, piece), :], x_recv.at[half, slot]).wait()
            lane = lax.broadcasted_iota(jnp.int32, (1, 2 * piece), 1)
            for quad in range(4):
                for pair in range(quarter // 2):
                    even = posb[quad * quarter + 2 * pair, pl.ds(half, 1), :]
                    odd = posb[quad * quarter + 2 * pair + 1, pl.ds(half, 1), :]
                    prow[quad, :, pl.ds(pair * 2 * piece, 2 * piece)] = jnp.broadcast_to(jnp.where(lane < piece, even, odd), (8, 2 * piece))
            for idx in range(2):
                for pair in range(quarter // 2):
                    line = prow[quarter_of(core, idx), pl.ds(0, 1), pl.ds(pair * 2 * piece, 2 * piece)]
                    column = jnp.broadcast_to(line, (2 * piece, 2 * piece)).T
                    rows = pl.ds(idx * q_len + pair * 2 * piece, 2 * piece)
                    pcol[rows, :] = column
                    angle = column * inv_freq[...]
                    cos_b[rows, :] = jnp.cos(angle)
                    sin_b[rows, :] = jnp.sin(angle)

        def norm_in(step, inner):
            rows = pl.ds(pl.multiple_of(step * 32, 32), 32)
            ab[rows, :] = rms(xb[half, rows, :].astype(F32), scales[layer, pl.ds(0, 1), :])
            return inner

        lax.fori_loop(0, n_tok // 32, norm_in, 0)

        q_wide = n_heads * HEAD_DIM
        for idx in range(2):
            rows = pl.ds(idx * q_len, q_len)
            home = pl.ds(pl.multiple_of(quarter_of(core, idx) * q_len, q_len), q_len)
            kv = dot(ab[rows, :], w_qkv[layer, :, q_wide:])
            low, high = rope(kv[:, :HEAD_DIM], cos_b[rows, :], sin_b[rows, :])
            kb[kv_slot, home, pl.ds(0, HALF_DIM)] = low.astype(BF16)
            kb[kv_slot, home, pl.ds(HALF_DIM, HALF_DIM)] = high.astype(BF16)
            vb[kv_slot, home, :] = kv[:, HEAD_DIM:].astype(BF16)
        for idx in range(2):
            for which in range(2):
                kv_copy(kv_slot, idx, which).start()
        for idx in range(2):
            rows = pl.ds(idx * q_len, q_len)
            for head in range(n_heads):
                raw = dot(ab[rows, :], w_qkv[layer, :, pl.ds(head * HEAD_DIM, HEAD_DIM)])
                low, high = rope(raw, cos_b[rows, :], sin_b[rows, :])
                there = pl.ds(head * q_len, q_len)
                qs[idx, there, pl.ds(0, HALF_DIM)] = (low * HEAD_DIM ** -0.5).astype(BF16)
                qs[idx, there, pl.ds(HALF_DIM, HALF_DIM)] = (high * HEAD_DIM ** -0.5).astype(BF16)
        for idx in range(2):
            for which in range(2):
                theirs = pl.ds(pl.multiple_of(quarter_of(1 - core, idx) * q_len, q_len), q_len)
                buf = (kb, vb)[which]
                pltpu.make_async_remote_copy(
                    src_ref=buf.at[kv_slot, theirs, :], dst_ref=buf.at[kv_slot, theirs, :], send_sem=kv_send.at[kv_slot, idx, which],
                    recv_sem=kv_recv.at[kv_slot, idx, which], device_id={"cp": 2 * chip + 1 - core}, device_id_type=pl.DeviceIdType.MESH).wait_recv()

        centre = jnp.where(layer == 0, (WINDOW - 1) * 0.5, n_tok * 2.0 - 0.5)
        for idx in range(2):
            quad = quarter_of(core, idx)
            lowest = jnp.where(layer == 0, jnp.maximum(quad - WINDOW // q_len, 0), 0)
            oacc[...] = jnp.zeros_like(oacc)
            lacc[...] = jnp.zeros_like(lacc)

            def key_block(block, inner):
                keys = pl.ds(pl.multiple_of(block * q_len, q_len), q_len)
                k_tile = kb[kv_slot, keys, :]
                v_tile = vb[kv_slot, keys, :]
                here = pcol[pl.ds(idx * q_len, q_len), :] - centre
                there = prow[block, pl.ds(0, 1), :]
                seen = jnp.concatenate([jnp.abs(here - there[:, :HALF_DIM]) <= centre, jnp.abs(here - there[:, HALF_DIM:]) <= centre], axis=1)
                for head in range(n_heads):
                    rows = pl.ds(head * q_len, q_len)
                    scores = lax.dot_general(qs[idx, rows, :], k_tile, (((1,), (1,)), ((), ())), preferred_element_type=F32)
                    expd = jnp.where(seen, jnp.exp2((SOFT_CAP * LOG2E) * jnp.tanh(scores * (1.0 / SOFT_CAP))), 0.0)
                    lacc[rows, :] += expd[:, :HALF_DIM] + expd[:, HALF_DIM:]
                    oacc[rows, :] += dot(expd.astype(BF16), v_tile)
                return inner

            lax.fori_loop(lowest, quad + 1, key_block, 0)
            for head in range(n_heads):
                rows = pl.ds(head * q_len, q_len)
                total = jnp.sum(lacc[rows, :], axis=1, keepdims=True)
                ob[pl.ds(idx * q_len, q_len), pl.ds(head * HEAD_DIM, HEAD_DIM)] = (oacc[rows, :] / total).astype(BF16)

        acc[...] = dot(ob[...], w_o[layer])

        def norm_mid(step, inner):
            rows = pl.ds(pl.multiple_of(step * 16, 16), 16)
            attn = acc[rows, :].astype(BF16).astype(F32)
            mid = (xb[half, rows, :].astype(F32) + rms(attn, scales[layer, pl.ds(1, 1), :]).astype(F32)).astype(BF16)
            xb[half, rows, :] = mid
            ab[rows, :] = rms(mid.astype(F32), scales[layer, pl.ds(2, 1), :])
            acc[rows, :] = jnp.zeros((16, dim), F32)
            return inner

        lax.fori_loop(0, n_tok // 16, norm_mid, 0)

        def ffn_tile(tile, inner):
            now = count * n_tiles + tile
            buf = now % RING
            for copy in tile_copies(0, 0, buf):
                copy.wait()

            @pl.when(now + RING - 1 < 4 * n_tiles)
            def _():
                start_tile(now + RING - 1)

            hb[...] = gelu_times(dot(ab[...], w_g[buf]), dot(ab[...], w_u[buf]))
            acc[...] += dot(hb[...], w_d[buf])
            return inner

        lax.fori_loop(0, n_tiles, ffn_tile, 0)

        def norm_out(step, inner):
            rows = pl.ds(pl.multiple_of(step * 16, 16), 16)
            down = acc[rows, :].astype(BF16).astype(F32)
            xb[half, rows, :] = (xb[half, rows, :].astype(F32) + rms(down, scales[layer, pl.ds(3, 1), :]).astype(F32)).astype(BF16)
            return inner

        lax.fori_loop(0, n_tok // 16, norm_out, 0)
        for idx in range(2):
            for which in range(2):
                kv_copy(kv_slot, idx, which).wait_send()

        @pl.when(layer == 1)
        def _():
            for slot in range(slots):
                to_piece, copy = o_copy(half, slot)

                @pl.when(to_piece != me)
                def _():
                    copy.start()

                @pl.when(to_piece == me)
                def _():
                    pltpu.make_async_copy(xb.at[half, pl.ds(slot * piece, piece), :], out.at[half * n_chips + chip], o_recv.at[half, chip]).start()

        return carry

    lax.fori_loop(0, 4, stage, 0)

    for half in range(2):
        for slot in range(slots):
            to_piece, copy = o_copy(half, slot)

            @pl.when(to_piece != me)
            def _():
                copy.wait_send()
        for from_chip in range(n_chips):
            pltpu.make_async_copy(xb.at[half, pl.ds(0, piece), :], out.at[half * n_chips + from_chip], o_recv.at[half, from_chip]).wait()
        for shift in order:
            if shift:
                x_copy(half, shift).wait_send()
            else:
                @pl.when(my_core != core)
                def _():
                    x_copy(half, shift).wait_send()
    for shift in order:
        for to_core in range(2):
            if shift:
                p_copy(shift, to_core).wait_send()
            else:
                @pl.when(core != to_core)
                def _():
                    p_copy(shift, to_core).wait_send()


def solution(mesh):
    cp_size = mesh.shape["cp"]

    def device_step(hidden, positions, *weights):
        rows, piece, dim = hidden.shape
        n_chips = cp_size // 2
        n_tok = piece * cp_size // 2
        q_wide = weights[0].shape[1]
        ffn = weights[4].shape[1]
        n_heads = q_wide // HEAD_DIM
        q_len = n_tok // 2
        pos = positions.astype(F32).reshape(2, n_chips, piece).transpose(1, 0, 2)
        pos = jnp.pad(jnp.concatenate([pos, pos], axis=2), ((0, 0), (0, 6), (0, 0)))
        scales = 1.0 + jnp.stack([jnp.stack(weights[7:11]), jnp.stack(weights[18:22])])
        inv_freq = (THETA ** (-(jnp.arange(HALF_DIM, dtype=F32) * 2.0 / HEAD_DIM)))[None, :]
        matrices = weights[0:7] + weights[11:18]
        hbm = pl.BlockSpec(memory_space=pltpu.HBM)
        vmem = pl.BlockSpec(memory_space=pltpu.VMEM)
        scratch = [
            pltpu.VMEM((2, n_tok, dim), BF16),
            pltpu.VMEM((n_tok, dim), BF16),
            pltpu.VMEM((2, n_heads * q_len, HEAD_DIM), BF16),
            pltpu.VMEM((2, 2 * n_tok, HEAD_DIM), BF16),
            pltpu.VMEM((2, 2 * n_tok, HEAD_DIM), BF16),
            pltpu.VMEM((n_tok, q_wide), BF16),
            pltpu.VMEM((n_heads * q_len, HEAD_DIM), F32),
            pltpu.VMEM((n_heads * q_len, HALF_DIM), F32),
            pltpu.VMEM((cp_size, 8, 2 * piece), F32),
            pltpu.VMEM((n_tok, HALF_DIM), F32),
            pltpu.VMEM((4, 8, q_len), F32),
            pltpu.VMEM((n_tok, HALF_DIM), F32),
            pltpu.VMEM((n_tok, HALF_DIM), F32),
            pltpu.VMEM((n_tok, dim), F32),
            pltpu.VMEM((n_tok, F_TILE), BF16),
            pltpu.VMEM((2, dim, q_wide + 2 * HEAD_DIM), BF16),
            pltpu.VMEM((2, q_wide, dim), BF16),
            pltpu.VMEM((RING, dim, F_TILE), BF16),
            pltpu.VMEM((RING, dim, F_TILE), BF16),
            pltpu.VMEM((RING, F_TILE, dim), BF16),
            pltpu.SemaphoreType.DMA((2, 4)),
            pltpu.SemaphoreType.DMA((3, RING)),
            pltpu.SemaphoreType.DMA((2, n_chips)),
            pltpu.SemaphoreType.DMA((2, n_chips)),
            pltpu.SemaphoreType.DMA((n_chips, 2)),
            pltpu.SemaphoreType.DMA((cp_size,)),
            pltpu.SemaphoreType.DMA((2, 2, 2)),
            pltpu.SemaphoreType.DMA((2, 2, 2)),
            pltpu.SemaphoreType.DMA((2, n_chips)),
            pltpu.SemaphoreType.DMA((2, n_chips)),
        ]
        return pl.pallas_call(
            functools.partial(fused_kernel, cp_size),
            out_shape=jax.ShapeDtypeStruct(hidden.shape, BF16),
            in_specs=[hbm, hbm, vmem, vmem] + [hbm] * 14,
            out_specs=hbm,
            scratch_shapes=scratch,
            compiler_params=pltpu.CompilerParams(collective_id=0, has_side_effects=True, vmem_limit_bytes=62 * 2 ** 20),
            name="two_layers",
        )(hidden, pos, scales, inv_freq, *matrices)

    specs_in = tuple([P("dp", "cp"), P("dp", "cp")] + [P()] * 22)
    return jax.shard_map(device_step, mesh=mesh, in_specs=specs_in, out_specs=P("dp", "cp"), check_vma=False)
```

time: 743 us -> 283 us (0.38)
  Pallas kernels: 0 us -> 268 us
  matrix products: 218 us -> 0 us
  waiting for transfers between devices: 190 us -> 0 us
  starting transfers between devices: 141 us -> 0 us
  blocking collectives: 71.5 us -> 0 us
  local copies, waits for them, and re-layouts: 57.2 us -> 8.87 us
  other arithmetic: 41.1 us -> 2.57 us
  between operations: 14.4 us -> 0.02 us
    pallas_call x0 -> x1, Pallas kernels: none -> 268 us  [device_step(): pl.pallas_call(functools.partial(fused_kernel, cp_size), out_shape=jax.Sh...]
    dot_general x18 -> x0, matrix products: 218 us -> none  [the longest x2 56.5 us: finish_layer(): jnp.einsum('btd,df->btf', normed_mid, w_up, preferred_element_type=jnp.fl...]
    all_gather x2 -> x0, waiting for transfers between devices: 185 us -> none  [the longest x1 151 us: device_step(): key_all = lax.all_gather(key_rot, 'cp', axis=1, tiled=True)]
    ppermute x16 -> x0, starting transfers between devices: 140 us -> none  [the longest x8 101 us: device_step(): value_parts.append(lax.ppermute(value_t, 'cp', perm_pairs))]
    all_gather x1 -> x0, blocking collectives: 71.5 us -> none  [device_step(): all_pos = lax.all_gather(positions, 'cp', axis=1, tiled=True)]
    convert_element_type x4 -> x0, local copies, waits for them, and re-layouts: 19.2 us -> none  [the longest x2 11.4 us: apply_rope(): widened = heads_in.astype(jnp.float32)]
    reduce_sum x6 -> x0, other arithmetic: 18.5 us -> none  [the longest x2 12.2 us: attend(): jax.nn.softmax(jnp.where(visible, capped, -1e+30), axis=-1)]
    unnamed x87 -> x1, local copies, waits for them, and re-layouts: 20.1 us -> 3.26 us
  transfers between devices with their start and end apart: 18 -> 0, of which waited for: 4 -> 0; matrix products, arithmetic and copies ran while one was open for 13% -> 0% of each run, Pallas kernels for 0% -> 0%
where the time goes in v1:
time: 283 us; the launch traced here: 279 us
  Pallas kernels  268 us (95%)
  local copies, waits for them, and re-layouts  8.87 us (3%)
    pallas_call x1, Pallas kernels, device_step(): pl.pallas_call(functools.partial(fused_kernel, cp_size), out_shape=jax.Sh...  268 us

profile of v1, /device:TPU:21, one launch (start us, length us, event | category | flops | bytes accessed | tf_op | source)
XLA Modules:
  0.0 279.1 jit_solution(16205147396925835733)
XLA Ops:
  0.0 0.5 negate_power_fusion.inv_freq
  0.5 0.7 stack.39
  1.2 0.7 stack.40
  1.9 0.7 stack.41
  2.6 0.7 stack.42
  3.3 0.7 stack.45
  4.0 0.7 stack.46
  4.7 0.7 stack.47
  5.4 0.7 stack.48
  6.2 0.6 maximum_add_fusion.scales
  6.8 0.7 convert_bitcast_fusion
  7.5 0.7 select_maximum_fusion.pos_rows
  8.2 267.6 %two_layers.1 = bf16[16,64,1152]{2,1,0:T(8,128)(2,1)} custom-call(bf16[16,64,1152]{2,1,0:T(8,128)(2,1)} %hidden.1, f32[8,8,128]{2,1,0:T(8,128)} %select_maximum_fusion.pos_rows, f32[2,4,1152]{2,1,0:T(4,128)} %maximum_add_fusion.scales, f32[1,128]{1,0:T(1,128)} %negate_power_fusion.inv_freq, bf16[1152,1024]{1,0:T(8,128)(2,1)} %refs_0_.1, ...), custom_call_target="tpu_custom_call" | custom-call | tf_op jit(solution)/shard_map/two_layers/pallas_call | solution.py:397
  275.8 3.3 %copy.29 = bf16[16,64,1152]{2,1,0:T(8,128)(2,1)} copy(bf16[16,64,1152]{2,1,0:T(8,128)(2,1)} %two_layers.1) | data formatting | bytes 4718592
  (2 shorter events, 0.0 us)

commit v2 on v1

v2 whole, which is shorter than its diff:
```python
import functools

import jax
import jax.numpy as jnp
import numpy as np
from jax import lax
from jax.experimental import pallas as pl
from jax.experimental.pallas import tpu as pltpu
from jax.sharding import PartitionSpec as P

HEAD_DIM = 256
HALF_DIM = HEAD_DIM // 2
WINDOW = 512
EPSILON = 1e-6
THETA = 10000.0
SOFT_CAP = 50.0
LOG2E = 1.4426950408889634
GELU_A = 0.7978845608028654
F_TILE = 2304
F_SUB = 768
BF16 = jnp.bfloat16
F32 = jnp.float32


def dot(lhs, rhs):
    return jnp.dot(lhs, rhs, preferred_element_type=F32)


def gelu_times(gate, up):
    gate = gate.astype(BF16).astype(F32)
    up = up.astype(BF16).astype(F32)
    inner = gate * (GELU_A + (GELU_A * 0.044715) * (gate * gate))
    scaled = (0.5 * gate) * up
    return (scaled + scaled * jnp.tanh(inner)).astype(BF16)


def rms(rows, scale):
    mean_sq = jnp.mean(rows * rows, axis=-1, keepdims=True)
    return (rows * lax.rsqrt(mean_sq + EPSILON) * scale).astype(BF16)


def rope(raw, cos_t, sin_t):
    raw = raw.astype(BF16).astype(F32)
    first, second = raw[:, :HALF_DIM], raw[:, HALF_DIM:]
    return first * cos_t - second * sin_t, second * cos_t + first * sin_t


def fused_kernel(cp_size, hidden, positions, inv_freq, *refs):
    raw_scales = (refs[0:4], refs[4:8])
    weights = (refs[8:15], refs[15:22])
    out = refs[22]
    (xb, ab, qs, kb, vb, ob, mid_b, mask_b, ptile, posb, pcol, prow, cos_b, sin_b, scales, acc, hb, w_qkv, w_o, w_g, w_u, w_d,
     w_sem, ring_sem, x_send, x_recv, p_send, p_recv, kv_send, kv_recv, o_send, o_recv) = refs[23:]
    n_chips = cp_size // 2
    piece = hidden.shape[1]
    dim = hidden.shape[2]
    n_tok = xb.shape[1]
    slots = n_tok // piece
    quarter = slots // 2
    q_len = n_tok // 2
    n_heads = w_o.shape[1] // HEAD_DIM
    q_wide = n_heads * HEAD_DIM
    n_tiles = weights[0][4].shape[1] // F_TILE
    me = lax.axis_index("cp")
    chip, core = me // 2, me % 2
    my_quarter = me // quarter
    my_core = jnp.where((my_quarter == 0) | (my_quarter == 3), 0, 1)
    my_slot = me % quarter + jnp.where(my_quarter >= 2, quarter, 0)

    def quarter_of(which_core, idx):
        return which_core + idx * (3 - 2 * which_core)

    def rows_of(start, size):
        return pl.ds(pl.multiple_of(start, size), size)

    w_copies = []
    for layer in range(2):
        wq, wk, wv, wo = weights[layer][:4]
        w_copies.append((
            pltpu.make_async_copy(wq, w_qkv.at[layer, :, pl.ds(0, q_wide)], w_sem.at[layer, 0]),
            pltpu.make_async_copy(wk, w_qkv.at[layer, :, pl.ds(q_wide, HEAD_DIM)], w_sem.at[layer, 1]),
            pltpu.make_async_copy(wv, w_qkv.at[layer, :, pl.ds(q_wide + HEAD_DIM, HEAD_DIM)], w_sem.at[layer, 2]),
            pltpu.make_async_copy(wo, w_o.at[layer], w_sem.at[layer, 3]),
        ))

    def tile_copies(layer, tile, buf):
        gate, up, down = weights[layer][4:7]
        cols = rows_of(tile * F_TILE, F_TILE)
        return (
            pltpu.make_async_copy(gate.at[:, cols], w_g.at[buf], ring_sem.at[0, buf]),
            pltpu.make_async_copy(up.at[:, cols], w_u.at[buf], ring_sem.at[1, buf]),
            pltpu.make_async_copy(down.at[cols, :], w_d.at[buf], ring_sem.at[2, buf]),
        )

    def start_tile(layer, tile, buf):
        for which in range(2):
            @pl.when(layer == which)
            def _():
                for copy in tile_copies(which, tile, buf):
                    copy.start()

    pos = positions[...].astype(F32)
    pos = jnp.concatenate([pos, pos], axis=1)
    for to_chip in range(n_chips):
        for half in range(2):
            row = half * n_chips + to_chip
            ptile[to_chip, pl.ds(half, 1), :] = pos[row:row + 1, :]
    for layer in range(2):
        for which in range(4):
            scales[layer * 4 + which] = 1.0 + raw_scales[layer][which][...]

    barrier = pltpu.get_barrier_semaphore()
    for shift in range(1, cp_size):
        pl.semaphore_signal(barrier, inc=1, device_id={"cp": lax.rem(me + shift, cp_size)}, device_id_type=pl.DeviceIdType.MESH)
    pl.semaphore_wait(barrier, cp_size - 1)

    def x_copy(half, to_chip):
        return pltpu.make_async_remote_copy(
            src_ref=hidden.at[half * n_chips + to_chip], dst_ref=xb.at[half, rows_of(my_slot * piece, piece), :],
            send_sem=x_send.at[half, to_chip], recv_sem=x_recv.at[half, my_slot],
            device_id={"cp": 2 * to_chip + my_core}, device_id_type=pl.DeviceIdType.MESH)

    def p_copy(to_chip, to_core):
        return pltpu.make_async_remote_copy(
            src_ref=ptile.at[to_chip], dst_ref=posb.at[me], send_sem=p_send.at[to_chip, to_core], recv_sem=p_recv.at[me],
            device_id={"cp": 2 * to_chip + to_core}, device_id_type=pl.DeviceIdType.MESH)

    def each_chip(parity):
        for step in (2, 1, 3, 0):
            yield 2 * lax.rem(chip // 2 + step, n_chips // 2) + parity

    def unless_me(target, copy_call, local_call):
        @pl.when(target != me)
        def _():
            copy_call()

        if local_call is not None:
            @pl.when(target == me)
            def _():
                local_call()

    for parity in range(2):
        for to_chip in each_chip(parity):
            for to_core in range(2):
                unless_me(2 * to_chip + to_core, lambda: p_copy(to_chip, to_core).start(),
                          lambda: pltpu.make_async_copy(ptile.at[to_chip], posb.at[me], p_recv.at[me]).start())
    for half in range(2):
        for parity in range(2):
            for to_chip in each_chip(parity):
                unless_me(2 * to_chip + my_core, lambda: x_copy(half, to_chip).start(),
                          lambda: pltpu.make_async_copy(hidden.at[half * n_chips + to_chip], xb.at[half, rows_of(my_slot * piece, piece), :], x_recv.at[half, my_slot]).start())

    for layer in range(2):
        for copy in w_copies[layer]:
            copy.start()
        start_tile(0, layer, layer)
    for from_piece in range(cp_size):
        pltpu.make_async_copy(ptile.at[0], posb.at[from_piece], p_recv.at[from_piece]).wait()
    for layer in range(2):
        for copy in w_copies[layer]:
            copy.wait()

    def kv_copy(slot, idx, which, owner):
        buf = (kb, vb)[which]
        rows = rows_of(quarter_of(owner, idx) * q_len, q_len)
        return pltpu.make_async_remote_copy(
            src_ref=buf.at[slot, rows, :], dst_ref=buf.at[slot, rows, :], send_sem=kv_send.at[slot, idx, which],
            recv_sem=kv_recv.at[slot, idx, which], device_id={"cp": 2 * chip + 1 - core}, device_id_type=pl.DeviceIdType.MESH)

    def o_target(idx, j):
        return quarter_of(core, idx) * quarter + j

    def o_copy(half, idx, j):
        slot = idx * quarter + j
        return pltpu.make_async_remote_copy(
            src_ref=xb.at[half, rows_of(slot * piece, piece), :], dst_ref=out.at[half * n_chips + chip],
            send_sem=o_send.at[half, slot], recv_sem=o_recv.at[half, chip],
            device_id={"cp": o_target(idx, j)}, device_id_type=pl.DeviceIdType.MESH)

    def stage(count, carry):
        half, layer = count // 2, count % 2
        kv_slot = count % 2

        @pl.when(layer == 0)
        def _():
            for slot in range(slots):
                pltpu.make_async_copy(hidden.at[0], xb.at[half, pl.ds(slot * piece, piece), :], x_recv.at[half, slot]).wait()
            lane = lax.broadcasted_iota(jnp.int32, (1, 2 * piece), 1)
            for quad in range(4):
                for pair in range(quarter // 2):
                    even = posb[quad * quarter + 2 * pair, pl.ds(half, 1), :]
                    odd = posb[quad * quarter + 2 * pair + 1, pl.ds(half, 1), :]
                    prow[quad, :, pl.ds(pair * 2 * piece, 2 * piece)] = jnp.broadcast_to(jnp.where(lane < piece, even, odd), (8, 2 * piece))
            for idx in range(2):
                for pair in range(quarter // 2):
                    line = prow[quarter_of(core, idx), pl.ds(0, 1), pl.ds(pair * 2 * piece, 2 * piece)]
                    column = jnp.broadcast_to(line, (2 * piece, 2 * piece)).T
                    rows = pl.ds(idx * q_len + pair * 2 * piece, 2 * piece)
                    pcol[rows, :] = column
                    angle = column * inv_freq[...]
                    cos_b[rows, :] = jnp.cos(angle)
                    sin_b[rows, :] = jnp.sin(angle)

        pre_att = scales[layer * 4]
        for step in range(n_tok // 16):
            rows = pl.ds(step * 16, 16)
            ab[rows, :] = rms(xb[half, rows, :].astype(F32), pre_att)
        for idx in range(2):
            rows = pl.ds(idx * q_len, q_len)
            home = rows_of(quarter_of(core, idx) * q_len, q_len)
            kv = dot(ab[rows, :], w_qkv[layer, :, q_wide:])
            low, high = rope(kv[:, :HEAD_DIM], cos_b[rows, :], sin_b[rows, :])
            kb[kv_slot, home, pl.ds(0, HALF_DIM)] = low.astype(BF16)
            kb[kv_slot, home, pl.ds(HALF_DIM, HALF_DIM)] = high.astype(BF16)
            vb[kv_slot, home, :] = kv[:, HEAD_DIM:].astype(BF16)
        for idx in range(2):
            for which in range(2):
                kv_copy(kv_slot, idx, which, core).start()
        for idx in range(2):
            rows = pl.ds(idx * q_len, q_len)
            for head in range(n_heads):
                raw = dot(ab[rows, :], w_qkv[layer, :, pl.ds(head * HEAD_DIM, HEAD_DIM)])
                low, high = rope(raw, cos_b[rows, :], sin_b[rows, :])
                there = pl.ds(head * q_len, q_len)
                qs[idx, there, pl.ds(0, HALF_DIM)] = (low * HEAD_DIM ** -0.5).astype(BF16)
                qs[idx, there, pl.ds(HALF_DIM, HALF_DIM)] = (high * HEAD_DIM ** -0.5).astype(BF16)

        pairs = ((0, 0), (1 - core, 1), (1, jnp.where(core == 0, 2, 0)), (1, jnp.where(core == 0, 3, 1)), (1, jnp.where(core == 0, 0, 2)))
        centre = jnp.where(layer == 0, (WINDOW - 1) * 0.5, n_tok * 2.0 - 0.5)
        for number, (idx, block) in enumerate(pairs):
            here = pcol[rows_of(idx * q_len, q_len), :] - centre
            there = prow[block, pl.ds(0, 1), :]
            for part in range(2):
                lanes = pl.ds(part * HALF_DIM, HALF_DIM)
                seen = jnp.abs(here - there[:, part * HALF_DIM:(part + 1) * HALF_DIM]) <= centre
                mask_b[number, :, lanes] = jnp.where(seen, 1.0, 0.0)
        for idx in range(2):
            for which in range(2):
                kv_copy(kv_slot, idx, which, 1 - core).wait_recv()
        to_first = jnp.where(core == 1, 1.0, 0.0)
        to_second = 1.0 - to_first
        for head in range(n_heads):
            sums, values = [], []
            for number, (idx, block) in enumerate(pairs):
                keys = rows_of(block * q_len, q_len)
                scores = lax.dot_general(qs[idx, pl.ds(head * q_len, q_len), :], kb[kv_slot, keys, :], (((1,), (1,)), ((), ())), preferred_element_type=F32)
                expd = jnp.exp2((SOFT_CAP * LOG2E) * jnp.tanh(scores * (1.0 / SOFT_CAP))) * mask_b[number]
                sums.append(expd[:, :HALF_DIM] + expd[:, HALF_DIM:])
                values.append(dot(expd.astype(BF16), vb[kv_slot, keys, :]))
            totals = (sums[0] + to_first * sums[1], (sums[2] + sums[3] + sums[4]) + to_second * sums[1])
            mixed = (values[0] + to_first * values[1], (values[2] + values[3] + values[4]) + to_second * values[1])
            for idx in range(2):
                share = 1.0 / jnp.sum(totals[idx], axis=1, keepdims=True)
                ob[pl.ds(idx * q_len, q_len), pl.ds(head * HEAD_DIM, HEAD_DIM)] = (mixed[idx] * share).astype(BF16)

        post_att, pre_ffw = scales[layer * 4 + 1], scales[layer * 4 + 2]
        for idx in range(2):
            rows = pl.ds(idx * q_len, q_len)
            mid_b[rows, :] = dot(ob[rows, :], w_o[layer])
        for step in range(n_tok // 16):
            rows = pl.ds(step * 16, 16)
            attn = mid_b[rows, :].astype(BF16).astype(F32)
            mid = (xb[half, rows, :].astype(F32) + rms(attn, post_att).astype(F32)).astype(BF16)
            xb[half, rows, :] = mid
            ab[rows, :] = rms(mid.astype(F32), pre_ffw)

        even = count % 2
        post_ffw = scales[layer * 4 + 3]

        def ffn_part(part, inner):
            idx = jnp.where(chip < n_chips // 2, 1 - part, part)
            rows = rows_of(idx * q_len, q_len)
            acc[...] = jnp.zeros_like(acc)

            def ffn_tile(step, inner2):
                buf = (even + step) % 2

                @pl.when((part == 0) | (step == n_tiles - 1))
                def _():
                    for copy in tile_copies(0, 0, buf):
                        copy.wait()

                for sub in range(F_TILE // F_SUB):
                    cols = pl.ds(sub * F_SUB, F_SUB)
                    hb[:, cols] = gelu_times(dot(ab[rows, :], w_g[buf, :, cols]), dot(ab[rows, :], w_u[buf, :, cols]))
                acc[...] += dot(hb[...], w_d[buf])

                @pl.when(step == 0)
                def _():
                    start_tile(layer, (1 - part) * (n_tiles - 1), buf)

                @pl.when((part == 1) & (step > 0) & (count < 3))
                def _():
                    start_tile(1 - layer, step - 1, buf)

                return inner2

            lax.fori_loop(0, n_tiles, ffn_tile, 0)
            for step in range(q_len // 16):
                those = rows_of(idx * q_len + step * 16, 16)
                down = acc[pl.ds(step * 16, 16), :].astype(BF16).astype(F32)
                xb[half, those, :] = (xb[half, those, :].astype(F32) + rms(down, post_ffw).astype(F32)).astype(BF16)

            @pl.when(layer == 1)
            def _():
                for j in range(quarter):
                    unless_me(o_target(idx, j), lambda: o_copy(half, idx, j).start(),
                              lambda: pltpu.make_async_copy(xb.at[half, rows_of((idx * quarter + j) * piece, piece), :], out.at[half * n_chips + chip], o_recv.at[half, chip]).start())

            return inner

        lax.fori_loop(0, 2, ffn_part, 0)
        for idx in range(2):
            for which in range(2):
                kv_copy(kv_slot, idx, which, core).wait_send()
        return carry

    lax.fori_loop(0, 4, stage, 0)

    for half in range(2):
        for idx in range(2):
            for j in range(quarter):
                unless_me(o_target(idx, j), lambda: o_copy(half, idx, j).wait_send(), None)
        for from_chip in range(n_chips):
            pltpu.make_async_copy(xb.at[half, pl.ds(0, piece), :], out.at[half * n_chips + from_chip], o_recv.at[half, from_chip]).wait()
        for to_chip in range(n_chips):
            unless_me(2 * to_chip + my_core, lambda: x_copy(half, to_chip).wait_send(), None)
    for to_chip in range(n_chips):
        for to_core in range(2):
            unless_me(2 * to_chip + to_core, lambda: p_copy(to_chip, to_core).wait_send(), None)


def solution(mesh):
    cp_size = mesh.shape["cp"]

    def device_step(hidden, positions, *weights):
        rows, piece, dim = hidden.shape
        n_chips = cp_size // 2
        n_tok = piece * cp_size // 2
        q_wide = weights[0].shape[1]
        n_heads = q_wide // HEAD_DIM
        q_len = n_tok // 2
        inv_freq = (THETA ** (-(np.arange(HALF_DIM) * 2.0 / HEAD_DIM))).astype(np.float32)[None, :]
        scales = [w[None, :] for w in weights[7:11] + weights[18:22]]
        matrices = weights[0:7] + weights[11:18]
        hbm = pl.BlockSpec(memory_space=pltpu.HBM)
        vmem = pl.BlockSpec(memory_space=pltpu.VMEM)
        scratch = [
            pltpu.VMEM((2, n_tok, dim), BF16),
            pltpu.VMEM((n_tok, dim), BF16),
            pltpu.VMEM((2, n_heads * q_len, HEAD_DIM), BF16),
            pltpu.VMEM((2, 2 * n_tok, HEAD_DIM), BF16),
            pltpu.VMEM((2, 2 * n_tok, HEAD_DIM), BF16),
            pltpu.VMEM((n_tok, q_wide), BF16),
            pltpu.VMEM((n_tok, dim), F32),
            pltpu.VMEM((5, q_len, q_len), F32),
            pltpu.VMEM((n_chips, 8, 2 * piece), F32),
            pltpu.VMEM((cp_size, 8, 2 * piece), F32),
            pltpu.VMEM((n_tok, HALF_DIM), F32),
            pltpu.VMEM((4, 8, q_len), F32),
            pltpu.VMEM((n_tok, HALF_DIM), F32),
            pltpu.VMEM((n_tok, HALF_DIM), F32),
            pltpu.VMEM((8, 1, dim), F32),
            pltpu.VMEM((q_len, dim), F32),
            pltpu.VMEM((q_len, F_TILE), BF16),
            pltpu.VMEM((2, dim, q_wide + 2 * HEAD_DIM), BF16),
            pltpu.VMEM((2, q_wide, dim), BF16),
            pltpu.VMEM((2, dim, F_TILE), BF16),
            pltpu.VMEM((2, dim, F_TILE), BF16),
            pltpu.VMEM((2, F_TILE, dim), BF16),
            pltpu.SemaphoreType.DMA((2, 4)),
            pltpu.SemaphoreType.DMA((3, 2)),
            pltpu.SemaphoreType.DMA((2, n_chips)),
            pltpu.SemaphoreType.DMA((2, n_chips)),
            pltpu.SemaphoreType.DMA((n_chips, 2)),
            pltpu.SemaphoreType.DMA((cp_size,)),
            pltpu.SemaphoreType.DMA((2, 2, 2)),
            pltpu.SemaphoreType.DMA((2, 2, 2)),
            pltpu.SemaphoreType.DMA((2, n_chips)),
            pltpu.SemaphoreType.DMA((2, n_chips)),
        ]
        return pl.pallas_call(
            functools.partial(fused_kernel, cp_size),
            out_shape=jax.ShapeDtypeStruct(hidden.shape, BF16),
            in_specs=[hbm] + [vmem] * 10 + [hbm] * 14,
            out_specs=hbm,
            scratch_shapes=scratch,
            compiler_params=pltpu.CompilerParams(collective_id=0, has_side_effects=True, vmem_limit_bytes=67043328),
            name="two_layers",
        )(hidden, positions, inv_freq, *scales, *matrices)

    specs_in = tuple([P("dp", "cp"), P("dp", "cp")] + [P()] * 22)
    return jax.shard_map(device_step, mesh=mesh, in_specs=specs_in, out_specs=P("dp", "cp"), check_vma=False)
```

time: 283 us -> 224 us (0.79)
  Pallas kernels: 268 us -> 209 us
  local copies, waits for them, and re-layouts: 8.87 us -> 13.6 us
    pallas_call x1, Pallas kernels: 268 us -> 209 us  [device_step(): pl.pallas_call(functools.partial(fused_kernel, cp_size), out_shape=jax.Sh...]
    broadcast_in_dim x0 -> x8, local copies, waits for them, and re-layouts: none -> 10.3 us  [device_step(): scales = [w[None, :] for w in weights[7:11] + weights[18:22]]]
    another operation x8 -> x0, local copies, waits for them, and re-layouts: 5.6 us -> none  [the longest x4 2.8 us: device_step(): jnp.stack(weights[7:11])]
where the time goes in v2:
time: 224 us; the launch traced here: 222 us
  Pallas kernels  209 us (93%)
  local copies, waits for them, and re-layouts  13.6 us (6%)
    pallas_call x1, Pallas kernels, device_step(): pl.pallas_call(functools.partial(fused_kernel, cp_size), out_shape=jax.Sh...  209 us
    broadcast_in_dim x8, local copies, waits for them, and re-layouts, device_step(): scales = [w[None, :] for w in weights[7:11] + weights[18:22]]  10.3 us

profile of v2, /device:TPU:21, one launch (start us, length us, event | category | flops | bytes accessed | tf_op | source)
XLA Modules:
  0.0 222.4 jit_solution(2544371693995234777)
XLA Ops:
  0.0 1.3 broadcast_in_dim.24.refs_0_
  1.3 1.3 broadcast_in_dim.25.refs_1_
  2.6 1.3 broadcast_in_dim.26.refs_2_
  3.9 1.3 broadcast_in_dim.27.refs_3_
  5.2 1.3 broadcast_in_dim.28.refs_4_
  6.4 1.3 broadcast_in_dim.29.refs_5_
  7.7 1.3 broadcast_in_dim.30.refs_6_
  9.0 1.3 broadcast_in_dim.31.refs_7_
  10.3 208.8 %two_layers.1 = bf16[16,64,1152]{2,1,0:T(8,128)(2,1)} custom-call(bf16[16,64,1152]{2,1,0:T(8,128)(2,1)} %hidden.1, s32[16,64]{1,0:T(8,128)} %positions.1, f32[1,128]{1,0:T(1,128)} %constant.2.clone.inv_freq, f32[1,1152]{1,0:T(1,128)} %broadcast_in_dim.24.refs_0_, f32[1,1152]{1,0:T(1,128)} %broadcast_in_dim.25.refs_1_, f32[1,1152]{1,0:T(1,128)} %broadcast_in_dim.26.refs_2_, ...), custom_call_target="tpu_custom_call" | custom-call | tf_op jit(solution)/shard_map/two_layers/pallas_call | solution.py:382
  219.1 3.3 %copy.27 = bf16[16,64,1152]{2,1,0:T(8,128)(2,1)} copy(bf16[16,64,1152]{2,1,0:T(8,128)(2,1)} %two_layers.1) | data formatting | bytes 4718592

commit v3 on v2

v3 whole, which is shorter than its diff:
```python
import functools

import jax
import jax.numpy as jnp
import numpy as np
from jax import lax
from jax.experimental import pallas as pl
from jax.experimental.pallas import tpu as pltpu
from jax.sharding import PartitionSpec as P

HEAD_DIM = 256
HALF_DIM = HEAD_DIM // 2
WINDOW = 512
EPSILON = 1e-6
THETA = 10000.0
SOFT_CAP = 50.0
LOG2E = 1.4426950408889634
GELU_A = 0.7978845608028654
F_TILE = 2304
F_SUB = 256
GROUP = 64
BF16 = jnp.bfloat16
F32 = jnp.float32


def dot(lhs, rhs):
    return jnp.dot(lhs, rhs, preferred_element_type=F32)


def gelu_times(gate, up):
    gate = gate.astype(BF16).astype(F32)
    up = up.astype(BF16).astype(F32)
    inner = gate * (GELU_A + (GELU_A * 0.044715) * (gate * gate))
    scaled = (0.5 * gate) * up
    return (scaled + scaled * jnp.tanh(inner)).astype(BF16)


def rms(rows, scale):
    mean_sq = jnp.mean(rows * rows, axis=-1, keepdims=True)
    return (rows * lax.rsqrt(mean_sq + EPSILON) * scale).astype(BF16)


def rope(raw, cos_t, sin_t):
    raw = raw.astype(BF16).astype(F32)
    first, second = raw[:, :HALF_DIM], raw[:, HALF_DIM:]
    return first * cos_t - second * sin_t, second * cos_t + first * sin_t


def fused_kernel(cp_size, hidden, positions, inv_freq, *refs):
    raw_scales = (refs[0:4], refs[4:8])
    weights = (refs[8:15], refs[15:22])
    out = refs[22]
    (xb, ab, mb, qs, kb, vb, ob, mid_b, sum_b, mask_b, ptile, posb, pcol, prow, cos_b, sin_b, scales, acc, hb, w_qkv, w_o, w_g, w_u, w_d,
     w_sem, ring_sem, x_send, x_recv, p_send, p_recv, kv_send, kv_recv, o_send, o_recv) = refs[23:]
    n_chips = cp_size // 2
    piece = hidden.shape[1]
    dim = hidden.shape[2]
    n_tok = xb.shape[1]
    slots = n_tok // piece
    quarter = slots // 2
    q_len = n_tok // 2
    n_heads = w_o.shape[0] // HEAD_DIM
    q_wide = n_heads * HEAD_DIM
    me = lax.axis_index("cp")
    chip, core = me // 2, me % 2
    my_quarter = me // quarter
    my_core = jnp.where((my_quarter == 0) | (my_quarter == 3), 0, 1)
    my_slot = me % quarter + jnp.where(my_quarter >= 2, quarter, 0)

    def quarter_of(which_core, idx):
        return which_core + idx * (3 - 2 * which_core)

    def rows_of(start, size):
        return pl.ds(pl.multiple_of(start, size), size)

    def attention_weights(layer):
        wq, wk, wv, wo = weights[layer][:4]
        return (
            pltpu.make_async_copy(wq, w_qkv.at[:, pl.ds(0, q_wide)], w_sem.at[0]),
            pltpu.make_async_copy(wk, w_qkv.at[:, pl.ds(q_wide, HEAD_DIM)], w_sem.at[1]),
            pltpu.make_async_copy(wv, w_qkv.at[:, pl.ds(q_wide + HEAD_DIM, HEAD_DIM)], w_sem.at[2]),
            pltpu.make_async_copy(wo, w_o, w_sem.at[3]),
        )

    def tile_copies(layer, tile, buf):
        gate, up, down = weights[layer][4:7]
        cols = rows_of(tile * F_TILE, F_TILE)
        return (
            pltpu.make_async_copy(gate.at[:, cols], w_g.at[buf], ring_sem.at[0, buf]),
            pltpu.make_async_copy(up.at[:, cols], w_u.at[buf], ring_sem.at[1, buf]),
            pltpu.make_async_copy(down.at[cols, :], w_d.at[buf], ring_sem.at[2, buf]),
        )

    def start_tile(layer, tile, buf):
        for which in range(2):
            @pl.when(layer == which)
            def _():
                for copy in tile_copies(which, tile, buf):
                    copy.start()

    pos = positions[...].astype(F32)
    pos = jnp.concatenate([pos, pos], axis=1)
    for to_chip in range(n_chips):
        for half in range(2):
            row = half * n_chips + to_chip
            ptile[to_chip, pl.ds(half, 1), :] = pos[row:row + 1, :]
    for layer in range(2):
        for which in range(4):
            scales[layer * 4 + which] = 1.0 + raw_scales[layer][which][...].reshape(1, dim)

    barrier = pltpu.get_barrier_semaphore()
    for shift in range(1, cp_size):
        pl.semaphore_signal(barrier, inc=1, device_id={"cp": lax.rem(me + shift, cp_size)}, device_id_type=pl.DeviceIdType.MESH)
    pl.semaphore_wait(barrier, cp_size - 1)

    def x_copy(half, to_chip):
        return pltpu.make_async_remote_copy(
            src_ref=hidden.at[half * n_chips + to_chip], dst_ref=xb.at[half, rows_of(my_slot * piece, piece), :],
            send_sem=x_send.at[half, to_chip], recv_sem=x_recv.at[half, my_slot],
            device_id={"cp": 2 * to_chip + my_core}, device_id_type=pl.DeviceIdType.MESH)

    def p_copy(to_chip, to_core):
        return pltpu.make_async_remote_copy(
            src_ref=ptile.at[to_chip], dst_ref=posb.at[me], send_sem=p_send.at[to_chip, to_core], recv_sem=p_recv.at[me],
            device_id={"cp": 2 * to_chip + to_core}, device_id_type=pl.DeviceIdType.MESH)

    def each_chip(parity):
        for step in (2, 1, 3, 0):
            yield 2 * lax.rem(chip // 2 + step, n_chips // 2) + parity

    def unless_me(target, copy_call, local_call):
        @pl.when(target != me)
        def _():
            copy_call()

        if local_call is not None:
            @pl.when(target == me)
            def _():
                local_call()

    for parity in range(2):
        for to_chip in each_chip(parity):
            for to_core in range(2):
                unless_me(2 * to_chip + to_core, lambda: p_copy(to_chip, to_core).start(),
                          lambda: pltpu.make_async_copy(ptile.at[to_chip], posb.at[me], p_recv.at[me]).start())
    for half in range(2):
        for parity in range(2):
            for to_chip in each_chip(parity):
                unless_me(2 * to_chip + my_core, lambda: x_copy(half, to_chip).start(),
                          lambda: pltpu.make_async_copy(hidden.at[half * n_chips + to_chip], xb.at[half, rows_of(my_slot * piece, piece), :], x_recv.at[half, my_slot]).start())

    for copy in attention_weights(0):
        copy.start()
    for buf in range(2):
        start_tile(0, buf, buf)
    for from_piece in range(cp_size):
        pltpu.make_async_copy(ptile.at[0], posb.at[from_piece], p_recv.at[from_piece]).wait()
    for copy in attention_weights(0):
        copy.wait()

    def kv_copy(slot, idx, which, owner):
        buf = (kb, vb)[which]
        rows = rows_of(quarter_of(owner, idx) * q_len, q_len)
        return pltpu.make_async_remote_copy(
            src_ref=buf.at[slot, rows, :], dst_ref=buf.at[slot, rows, :], send_sem=kv_send.at[slot, idx, which],
            recv_sem=kv_recv.at[slot, idx, which], device_id={"cp": 2 * chip + 1 - core}, device_id_type=pl.DeviceIdType.MESH)

    def o_target(idx, j):
        return quarter_of(core, idx) * quarter + j

    def o_copy(half, idx, j):
        slot = idx * quarter + j
        return pltpu.make_async_remote_copy(
            src_ref=xb.at[half, rows_of(slot * piece, piece), :], dst_ref=out.at[half * n_chips + chip],
            send_sem=o_send.at[half, slot], recv_sem=o_recv.at[half, chip],
            device_id={"cp": o_target(idx, j)}, device_id_type=pl.DeviceIdType.MESH)

    def take_half(half):
        for slot in range(slots):
            pltpu.make_async_copy(hidden.at[0], xb.at[half, pl.ds(slot * piece, piece), :], x_recv.at[half, slot]).wait()
        lane = lax.broadcasted_iota(jnp.int32, (1, 2 * piece), 1)
        for quad in range(4):
            for pair in range(quarter // 2):
                even = posb[quad * quarter + 2 * pair, pl.ds(half, 1), :]
                odd = posb[quad * quarter + 2 * pair + 1, pl.ds(half, 1), :]
                prow[half, quad, :, pl.ds(pair * 2 * piece, 2 * piece)] = jnp.broadcast_to(jnp.where(lane < piece, even, odd), (8, 2 * piece))
        for idx in range(2):
            for pair in range(quarter // 2):
                line = prow[half, quarter_of(core, idx), pl.ds(0, 1), pl.ds(pair * 2 * piece, 2 * piece)]
                column = jnp.broadcast_to(line, (2 * piece, 2 * piece)).T
                rows = pl.ds(idx * q_len + pair * 2 * piece, 2 * piece)
                pcol[half, rows, :] = column
                angle = column * inv_freq[...]
                cos_b[half, rows, :] = jnp.cos(angle)
                sin_b[half, rows, :] = jnp.sin(angle)

    idx_rows = (pl.ds(0, q_len), pl.ds(q_len, q_len))
    mine = (quarter_of(core, 0), quarter_of(core, 1))
    pairs = ((0, mine[0]), (1, mine[1]), (1, mine[0]), (1 - core, jnp.where(core == 0, 1, 0)), (1, jnp.where(core == 0, 2, 0)))
    to_first = jnp.where(core == 1, 1.0, 0.0)
    to_second = 1.0 - to_first

    def steps_keys(layer, half):
        pre_att = scales[layer * 4]

        def norm_in(group):
            for step in range(group * GROUP, (group + 1) * GROUP, 16):
                rows = pl.ds(step, 16)
                ab[rows, :] = rms(xb[half, rows, :].astype(F32), pre_att)

        def make_keys(idx):
            home = rows_of(mine[idx] * q_len, q_len)
            kv = dot(ab[idx_rows[idx], :], w_qkv[:, q_wide:])
            low, high = rope(kv[:, :HEAD_DIM], cos_b[half, idx_rows[idx], :], sin_b[half, idx_rows[idx], :])
            kb[half, home, pl.ds(0, HALF_DIM)] = low.astype(BF16)
            kb[half, home, pl.ds(HALF_DIM, HALF_DIM)] = high.astype(BF16)
            vb[half, home, :] = kv[:, HEAD_DIM:].astype(BF16)

        def make_mask(number):
            idx, block = pairs[number]
            centre = jnp.where(layer == 0, (WINDOW - 1) * 0.5, n_tok * 2.0 - 0.5)
            here = pcol[half, rows_of(idx * q_len, q_len), :] - centre
            there = prow[half, block, pl.ds(0, 1), :]
            for part in range(2):
                lanes = pl.ds(part * HALF_DIM, HALF_DIM)
                seen = jnp.abs(here - there[:, part * HALF_DIM:(part + 1) * HALF_DIM]) <= centre
                mask_b[number, :, lanes] = jnp.where(seen, 1.0, 0.0)

        groups = n_tok // GROUP
        return ([functools.partial(norm_in, g) for g in range(groups // 2)] + [functools.partial(make_keys, 0)]
                + [functools.partial(norm_in, g) for g in range(groups // 2, groups)] + [functools.partial(make_keys, 1)]
                + [functools.partial(make_mask, number) for number in range(5)])

    def score(half, unit):
        head, number = unit
        idx, block = pairs[number]
        return lax.dot_general(qs[idx, pl.ds(head * q_len, q_len), :], kb[half, rows_of(block * q_len, q_len), :],
                               (((1,), (1,)), ((), ())), preferred_element_type=F32)

    def weigh(half, unit, scores):
        head, number = unit
        idx, block = pairs[number]
        expd = jnp.exp2((SOFT_CAP * LOG2E) * jnp.tanh(scores * (1.0 / SOFT_CAP))) * mask_b[number]
        return expd[:, :HALF_DIM] + expd[:, HALF_DIM:], dot(expd.astype(BF16), vb[half, rows_of(block * q_len, q_len), :])

    def wide(head):
        return pl.ds(head * HEAD_DIM, HEAD_DIM)

    def unit_steps(half, units, before, last):
        state = {"found": []}

        def run(place):
            unit = units[place]
            for call in before.get(place, ()):
                call()
            scores = state["ahead"] if place else score(half, unit)
            if place + 1 < len(units):
                state["ahead"] = score(half, units[place + 1])
            state["found"].append(weigh(half, unit, scores))
            if place + 1 == len(units) or units[place + 1][0] != unit[0]:
                last(unit[0], state["found"])
                state["found"] = []

        return [functools.partial(run, place) for place in range(len(units))]

    def steps_own(layer, half):
        def make_query(head):
            for idx in range(2):
                raw = dot(ab[idx_rows[idx], :], w_qkv[:, wide(head)])
                low, high = rope(raw, cos_b[half, idx_rows[idx], :], sin_b[half, idx_rows[idx], :])
                there = pl.ds(head * q_len, q_len)
                qs[idx, there, pl.ds(0, HALF_DIM)] = (low * HEAD_DIM ** -0.5).astype(BF16)
                qs[idx, there, pl.ds(HALF_DIM, HALF_DIM)] = (high * HEAD_DIM ** -0.5).astype(BF16)

        def last(head, found):
            sum_b[head, idx_rows[0], :] = found[0][0]
            mid_b[idx_rows[0], wide(head)] = found[0][1]
            sum_b[head, idx_rows[1], :] = found[1][0] + found[2][0]
            mid_b[idx_rows[1], wide(head)] = found[1][1] + found[2][1]

        units = [(head, number) for head in range(n_heads) for number in range(3)]
        before = {3 * head: (functools.partial(make_query, head + 1),) for head in range(n_heads - 1)}
        return [functools.partial(make_query, 0)] + unit_steps(half, units, before, last)

    def steps_rest(layer, half):
        post_att, pre_ffw = scales[layer * 4 + 1], scales[layer * 4 + 2]

        def last(head, found):
            totals = (sum_b[head, idx_rows[0], :] + to_first * found[0][0], (sum_b[head, idx_rows[1], :] + found[1][0]) + to_second * found[0][0])
            mixed = (mid_b[idx_rows[0], wide(head)] + to_first * found[0][1], (mid_b[idx_rows[1], wide(head)] + found[1][1]) + to_second * found[0][1])
            for idx in range(2):
                share = 1.0 / jnp.sum(totals[idx], axis=1, keepdims=True)
                ob[idx_rows[idx], wide(head)] = (mixed[idx] * share).astype(BF16)

        def project(idx):
            mid_b[idx_rows[idx], pl.ds(0, dim)] = dot(ob[idx_rows[idx], :], w_o[...])

        def norm_mid(group):
            for step in range(group * GROUP, (group + 1) * GROUP, 16):
                rows = pl.ds(step, 16)
                attn = mid_b[rows, pl.ds(0, dim)].astype(BF16).astype(F32)
                mid = (xb[half, rows, :].astype(F32) + rms(attn, post_att).astype(F32)).astype(BF16)
                xb[half, rows, :] = mid
                ab[rows, :] = rms(mid.astype(F32), pre_ffw)

        units = [(head, number) for head in range(n_heads) for number in (3, 4)]
        groups = n_tok // GROUP
        return (unit_steps(half, units, {}, last) + [functools.partial(project, idx) for idx in range(2)]
                + [functools.partial(norm_mid, g) for g in range(groups)])

    def send_keys(half):
        for idx in range(2):
            for which in range(2):
                kv_copy(half, idx, which, core).start()

    def await_keys(half):
        for idx in range(2):
            for which in range(2):
                kv_copy(half, idx, which, 1 - core).wait_recv()

    def await_sent_keys(half):
        for idx in range(2):
            for which in range(2):
                kv_copy(half, idx, which, core).wait_send()

    late = jnp.where(core == 0, (chip == 3) | (chip >= 5), (chip == 0) | ((chip >= 4) & (chip <= 6))).astype(jnp.int32)

    def part_idx(part):
        return jnp.where(part == 1, late, 1 - late)

    def tile_steps(half, part, buf, start, size, first):
        rows = rows_of(part_idx(part) * q_len + start, size)
        where = pl.ds(0, size)
        there = pl.ds(start, size)

        def up(sub):
            cols = pl.ds(sub * F_SUB, F_SUB)
            hb[where, cols] = gelu_times(dot(mb[rows, :], w_g[buf, :, cols]), dot(mb[rows, :], w_u[buf, :, cols]))

        def down(cols):
            product = dot(hb[where, :], w_d[buf, :, cols])
            acc[part, there, cols] = product if first else acc[part, there, cols] + product

        return ([functools.partial(up, sub) for sub in range(F_TILE // F_SUB)]
                + [functools.partial(down, pl.ds(0, dim // 512 * 256)), functools.partial(down, pl.ds(dim // 512 * 256, dim - dim // 512 * 256))])

    def weave(steps, more):
        done = 0
        for place, step in enumerate(steps):
            step()
            upto = (place + 1) * len(more) // len(steps)
            for other in more[done:upto]:
                other()
            done = upto

    def out_steps(layer, half, part, start, size):
        post_ffw = scales[layer * 4 + 3]

        def norm_out(first_row):
            for step in range(first_row, first_row + min(GROUP, size), 16):
                those = rows_of(part_idx(part) * q_len + step, 16)
                down = acc[part, pl.ds(step, 16), :].astype(BF16).astype(F32)
                xb[half, those, :] = (xb[half, those, :].astype(F32) + rms(down, post_ffw).astype(F32)).astype(BF16)

        return [functools.partial(norm_out, row) for row in range(start, start + size, GROUP)]

    def send_out(half, part, pieces):
        idx = part_idx(part)
        for j in pieces:
            unless_me(o_target(idx, j), lambda: o_copy(half, idx, j).start(),
                      lambda: pltpu.make_async_copy(xb.at[half, rows_of((idx * quarter + j) * piece, piece), :], out.at[half * n_chips + chip], o_recv.at[half, chip]).start())

    def await_tile(buf):
        for copy in tile_copies(0, 0, buf):
            copy.wait()

    def run_all(steps):
        for step in steps:
            step()

    take_half(0)
    run_all(steps_keys(0, 0))
    send_keys(0)
    run_all(steps_own(0, 0))
    await_keys(0)
    run_all(steps_rest(0, 0))
    mb[...] = ab[...]
    await_sent_keys(0)
    last_stage = 3

    def stage(count, carry):
        layer, half = count // 2, count % 2
        after = count + 1
        next_layer, next_half = after // 2, after % 2

        def buf_of(step):
            return (layer + step) % 2

        acc[...] = jnp.zeros_like(acc)

        def plain_tile(number, inner):
            part, step = number // 3, number % 3

            @pl.when((half == 0) | (step == 2))
            def _():
                await_tile(buf_of(step))

            run_all(tile_steps(half, part, buf_of(step), 0, q_len, False))

            @pl.when(step == 0)
            def _():
                start_tile(layer, 2 - 2 * part, buf_of(0))

            @pl.when((count == last_stage) & (step == 2))
            def _():
                run_all(out_steps(layer, half, part, 0, q_len))
                send_out(half, part, range(quarter))

            return inner

        lax.fori_loop(0, jnp.where(count == last_stage, 6, 3), plain_tile, 0)

        @pl.when(count < last_stage)
        def _():
            @pl.when(after < 2)
            def _():
                take_half(next_half)

            @pl.when(after == 2)
            def _():
                for copy in attention_weights(1):
                    copy.wait()

            weave(tile_steps(half, 1, buf_of(0), 0, q_len, True), steps_keys(next_layer, next_half) + out_steps(layer, half, 0, 0, q_len))
            start_tile(layer, 0, buf_of(0))
            send_keys(next_half)

            @pl.when(layer == 1)
            def _():
                send_out(half, 0, range(quarter))

            weave(tile_steps(half, 1, buf_of(1), 0, q_len, False), steps_own(next_layer, next_half))

            @pl.when(count == 1)
            def _():
                start_tile(1, 0, buf_of(1))

            await_keys(next_half)
            await_tile(buf_of(2))
            weave(tile_steps(half, 1, buf_of(2), 0, q_len, False), steps_rest(next_layer, next_half))

            @pl.when(count == 1)
            def _():
                start_tile(1, 1, buf_of(2))

            @pl.when(count == 0)
            def _():
                for copy in attention_weights(1):
                    copy.start()

            run_all(out_steps(layer, half, 1, 0, q_len))
            mb[...] = ab[...]
            await_sent_keys(next_half)

            @pl.when(layer == 1)
            def _():
                send_out(half, 1, range(quarter))

        return carry

    lax.fori_loop(0, 4, stage, 0)

    for half in range(2):
        for idx in range(2):
            for j in range(quarter):
                unless_me(o_target(idx, j), lambda: o_copy(half, idx, j).wait_send(), None)
        for from_chip in range(n_chips):
            pltpu.make_async_copy(xb.at[half, pl.ds(0, piece), :], out.at[half * n_chips + from_chip], o_recv.at[half, from_chip]).wait()
        for to_chip in range(n_chips):
            unless_me(2 * to_chip + my_core, lambda: x_copy(half, to_chip).wait_send(), None)
    for to_chip in range(n_chips):
        for to_core in range(2):
            unless_me(2 * to_chip + to_core, lambda: p_copy(to_chip, to_core).wait_send(), None)


def solution(mesh):
    cp_size = mesh.shape["cp"]

    def device_step(hidden, positions, *weights):
        rows, piece, dim = hidden.shape
        n_chips = cp_size // 2
        n_tok = piece * cp_size // 2
        q_wide = weights[0].shape[1]
        n_heads = q_wide // HEAD_DIM
        q_len = n_tok // 2
        inv_freq = (THETA ** (-(np.arange(HALF_DIM) * 2.0 / HEAD_DIM))).astype(np.float32)[None, :]
        scales = weights[7:11] + weights[18:22]
        matrices = weights[0:7] + weights[11:18]
        hbm = pl.BlockSpec(memory_space=pltpu.HBM)
        vmem = pl.BlockSpec(memory_space=pltpu.VMEM)
        scratch = [
            pltpu.VMEM((2, n_tok, dim), BF16),
            pltpu.VMEM((n_tok, dim), BF16),
            pltpu.VMEM((n_tok, dim), BF16),
            pltpu.VMEM((2, n_heads * q_len, HEAD_DIM), BF16),
            pltpu.VMEM((2, 2 * n_tok, HEAD_DIM), BF16),
            pltpu.VMEM((2, 2 * n_tok, HEAD_DIM), BF16),
            pltpu.VMEM((n_tok, q_wide), BF16),
            pltpu.VMEM((n_tok, max(dim, q_wide)), F32),
            pltpu.VMEM((n_heads, n_tok, HALF_DIM), F32),
            pltpu.VMEM((5, q_len, q_len), F32),
            pltpu.VMEM((n_chips, 8, 2 * piece), F32),
            pltpu.VMEM((cp_size, 8, 2 * piece), F32),
            pltpu.VMEM((2, n_tok, HALF_DIM), F32),
            pltpu.VMEM((2, 4, 8, q_len), F32),
            pltpu.VMEM((2, n_tok, HALF_DIM), F32),
            pltpu.VMEM((2, n_tok, HALF_DIM), F32),
            pltpu.VMEM((8, 1, dim), F32),
            pltpu.VMEM((2, q_len, dim), F32),
            pltpu.VMEM((q_len, F_TILE), BF16),
            pltpu.VMEM((dim, q_wide + 2 * HEAD_DIM), BF16),
            pltpu.VMEM((q_wide, dim), BF16),
            pltpu.VMEM((2, dim, F_TILE), BF16),
            pltpu.VMEM((2, dim, F_TILE), BF16),
            pltpu.VMEM((2, F_TILE, dim), BF16),
            pltpu.SemaphoreType.DMA((4,)),
            pltpu.SemaphoreType.DMA((3, 2)),
            pltpu.SemaphoreType.DMA((2, n_chips)),
            pltpu.SemaphoreType.DMA((2, n_chips)),
            pltpu.SemaphoreType.DMA((n_chips, 2)),
            pltpu.SemaphoreType.DMA((cp_size,)),
            pltpu.SemaphoreType.DMA((2, 2, 2)),
            pltpu.SemaphoreType.DMA((2, 2, 2)),
            pltpu.SemaphoreType.DMA((2, n_chips)),
            pltpu.SemaphoreType.DMA((2, n_chips)),
        ]
        return pl.pallas_call(
            functools.partial(fused_kernel, cp_size),
            out_shape=jax.ShapeDtypeStruct(hidden.shape, BF16),
            in_specs=[hbm] + [vmem] * 10 + [hbm] * 14,
            out_specs=hbm,
            scratch_shapes=scratch,
            compiler_params=pltpu.CompilerParams(collective_id=0, has_side_effects=True, vmem_limit_bytes=67043328),
            name="two_layers",
        )(hidden, positions, inv_freq, *scales, *matrices)

    specs_in = tuple([P("dp", "cp"), P("dp", "cp")] + [P()] * 22)
    return jax.shard_map(device_step, mesh=mesh, in_specs=specs_in, out_specs=P("dp", "cp"), check_vma=False)
```

time: 224 us -> 209 us (0.933)
  local copies, waits for them, and re-layouts: 13.6 us -> 3.26 us
  Pallas kernels: 209 us -> 206 us
    broadcast_in_dim x8 -> x0, local copies, waits for them, and re-layouts: 10.3 us -> none  [device_step(): scales = [w[None, :] for w in weights[7:11] + weights[18:22]]]
    pallas_call x1, Pallas kernels: 209 us -> 206 us  [device_step(): pl.pallas_call(functools.partial(fused_kernel, cp_size), out_shape=jax.Sh...]
where the time goes in v3:
time: 209 us
  Pallas kernels  206 us (99%)
  local copies, waits for them, and re-layouts  3.26 us (2%)
    pallas_call x1, Pallas kernels, device_step(): pl.pallas_call(functools.partial(fused_kernel, cp_size), out_shape=jax.Sh...  206 us

profile of v3, /device:TPU:21, one launch (start us, length us, event | category | flops | bytes accessed | tf_op | source)
XLA Modules:
  0.0 208.9 jit_solution(5643533546240102345)
XLA Ops:
  0.0 205.7 %two_layers.1 = bf16[16,64,1152]{2,1,0:T(8,128)(2,1)} custom-call(bf16[16,64,1152]{2,1,0:T(8,128)(2,1)} %hidden.1, s32[16,64]{1,0:T(8,128)} %positions.1, f32[1,128]{1,0:T(1,128)} %constant.2.clone.inv_freq, f32[1152]{0:T(1024)} %refs_0_.1, f32[1152]{0:T(1024)} %refs_1_.1, f32[1152]{0:T(1024)} %refs_2_.1, f32[1152]{0:T(1024)} %refs_3_.1, f32[1152]{0:T(1024)} %refs_4_.1, ...), custom_call_target="tpu_custom_call" | custom-call | tf_op jit(solution)/shard_map/two_layers/pallas_call | solution.py:537
  205.7 3.3 %copy.27 = bf16[16,64,1152]{2,1,0:T(8,128)(2,1)} copy(bf16[16,64,1152]{2,1,0:T(8,128)(2,1)} %two_layers.1) | data formatting | bytes 4718592

commit v4 on v3

--- a/solution.py
+++ b/solution.py
@@ -46,12 +46,13 @@
     return first * cos_t - second * sin_t, second * cos_t + first * sin_t
 
 
-def fused_kernel(cp_size, hidden, positions, inv_freq, *refs):
-    raw_scales = (refs[0:4], refs[4:8])
+def fused_kernel(cp_size, hidden, positions, inv_freq_in, *refs):
     weights = (refs[8:15], refs[15:22])
     out = refs[22]
     (xb, ab, mb, qs, kb, vb, ob, mid_b, sum_b, mask_b, ptile, posb, pcol, prow, cos_b, sin_b, scales, acc, hb, w_qkv, w_o, w_g, w_u, w_d,
-     w_sem, ring_sem, x_send, x_recv, p_send, p_recv, kv_send, kv_recv, o_send, o_recv) = refs[23:]
+     w_sem, ring_sem, x_send, x_recv, p_send, p_recv, kv_send, kv_recv, o_send, o_recv) = refs[23:-11]
+    pos_in, inv_freq, small_sem = refs[-11:-8]
+    raw_scales = refs[-8:]
     n_chips = cp_size // 2
     piece = hidden.shape[1]
     dim = hidden.shape[2]
@@ -71,7 +72,7 @@
         return which_core + idx * (3 - 2 * which_core)
 
     def rows_of(start, size):
-        return pl.ds(pl.multiple_of(start, size), size)
+        return pl.ds(start if isinstance(start, int) else pl.multiple_of(start, size), size)
 
     def attention_weights(layer):
         wq, wk, wv, wo = weights[layer][:4]
@@ -98,19 +99,24 @@
                 for copy in tile_copies(which, tile, buf):
                     copy.start()
 
-    pos = positions[...].astype(F32)
+    small = [pltpu.make_async_copy(positions, pos_in, small_sem.at[0]), pltpu.make_async_copy(inv_freq_in, inv_freq, small_sem.at[1])]
+    small += [pltpu.make_async_copy(refs[which], raw_scales[which], small_sem.at[2 + which]) for which in range(8)]
+    for copy in small:
+        copy.start()
+    barrier = pltpu.get_barrier_semaphore()
+    for shift in range(1, cp_size):
+        pl.semaphore_signal(barrier, inc=1, device_id={"cp": lax.rem(me + shift, cp_size)}, device_id_type=pl.DeviceIdType.MESH)
+    for copy in attention_weights(0):
+        copy.start()
+    for buf in range(2):
+        start_tile(0, buf, buf)
+    small[0].wait()
+    pos = pos_in[...].astype(F32)
     pos = jnp.concatenate([pos, pos], axis=1)
     for to_chip in range(n_chips):
         for half in range(2):
             row = half * n_chips + to_chip
             ptile[to_chip, pl.ds(half, 1), :] = pos[row:row + 1, :]
-    for layer in range(2):
-        for which in range(4):
-            scales[layer * 4 + which] = 1.0 + raw_scales[layer][which][...].reshape(1, dim)
-
-    barrier = pltpu.get_barrier_semaphore()
-    for shift in range(1, cp_size):
-        pl.semaphore_signal(barrier, inc=1, device_id={"cp": lax.rem(me + shift, cp_size)}, device_id_type=pl.DeviceIdType.MESH)
     pl.semaphore_wait(barrier, cp_size - 1)
 
     def x_copy(half, to_chip):
@@ -125,7 +131,7 @@
             device_id={"cp": 2 * to_chip + to_core}, device_id_type=pl.DeviceIdType.MESH)
 
     def each_chip(parity):
-        for step in (2, 1, 3, 0):
+        for step in (0, 1, 3, 2):
             yield 2 * lax.rem(chip // 2 + step, n_chips // 2) + parity
 
     def unless_me(target, copy_call, local_call):
@@ -149,10 +155,10 @@
                 unless_me(2 * to_chip + my_core, lambda: x_copy(half, to_chip).start(),
                           lambda: pltpu.make_async_copy(hidden.at[half * n_chips + to_chip], xb.at[half, rows_of(my_slot * piece, piece), :], x_recv.at[half, my_slot]).start())
 
-    for copy in attention_weights(0):
-        copy.start()
-    for buf in range(2):
-        start_tile(0, buf, buf)
+    for copy in small[1:]:
+        copy.wait()
+    for which in range(8):
+        scales[which] = 1.0 + raw_scales[which][...].reshape(1, dim)
     for from_piece in range(cp_size):
         pltpu.make_async_copy(ptile.at[0], posb.at[from_piece], p_recv.at[from_piece]).wait()
     for copy in attention_weights(0):
@@ -234,7 +240,7 @@
     def score(half, unit):
         head, number = unit
         idx, block = pairs[number]
-        return lax.dot_general(qs[idx, pl.ds(head * q_len, q_len), :], kb[half, rows_of(block * q_len, q_len), :],
+        return lax.dot_general(qs[idx, rows_of(head * q_len, q_len), :], kb[half, rows_of(block * q_len, q_len), :],
                                (((1,), (1,)), ((), ())), preferred_element_type=F32)
 
     def weigh(half, unit, scores):
@@ -244,7 +250,7 @@
         return expd[:, :HALF_DIM] + expd[:, HALF_DIM:], dot(expd.astype(BF16), vb[half, rows_of(block * q_len, q_len), :])
 
     def wide(head):
-        return pl.ds(head * HEAD_DIM, HEAD_DIM)
+        return rows_of(head * HEAD_DIM, HEAD_DIM)
 
     def unit_steps(half, units, before, last):
         state = {"found": []}
@@ -257,18 +263,18 @@
             if place + 1 < len(units):
                 state["ahead"] = score(half, units[place + 1])
             state["found"].append(weigh(half, unit, scores))
-            if place + 1 == len(units) or units[place + 1][0] != unit[0]:
+            if place + 1 == len(units) or units[place + 1][0] is not unit[0]:
                 last(unit[0], state["found"])
                 state["found"] = []
 
         return [functools.partial(run, place) for place in range(len(units))]
 
-    def steps_own(layer, half):
+    def steps_own(layer, half, only=None):
         def make_query(head):
             for idx in range(2):
                 raw = dot(ab[idx_rows[idx], :], w_qkv[:, wide(head)])
                 low, high = rope(raw, cos_b[half, idx_rows[idx], :], sin_b[half, idx_rows[idx], :])
-                there = pl.ds(head * q_len, q_len)
+                there = rows_of(head * q_len, q_len)
                 qs[idx, there, pl.ds(0, HALF_DIM)] = (low * HEAD_DIM ** -0.5).astype(BF16)
                 qs[idx, there, pl.ds(HALF_DIM, HALF_DIM)] = (high * HEAD_DIM ** -0.5).astype(BF16)
 
@@ -278,11 +284,13 @@
             sum_b[head, idx_rows[1], :] = found[1][0] + found[2][0]
             mid_b[idx_rows[1], wide(head)] = found[1][1] + found[2][1]
 
+        if only is not None:
+            return [functools.partial(make_query, only)] + unit_steps(half, [(only, number) for number in range(3)], {}, last)
         units = [(head, number) for head in range(n_heads) for number in range(3)]
         before = {3 * head: (functools.partial(make_query, head + 1),) for head in range(n_heads - 1)}
         return [functools.partial(make_query, 0)] + unit_steps(half, units, before, last)
 
-    def steps_rest(layer, half):
+    def steps_rest(layer, half, only=None, heads=True):
         post_att, pre_ffw = scales[layer * 4 + 1], scales[layer * 4 + 2]
 
         def last(head, found):
@@ -305,6 +313,10 @@
 
         units = [(head, number) for head in range(n_heads) for number in (3, 4)]
         groups = n_tok // GROUP
+        if only is not None:
+            return unit_steps(half, [(only, 3), (only, 4)], {}, last)
+        if not heads:
+            units = []
         return (unit_steps(half, units, {}, last) + [functools.partial(project, idx) for idx in range(2)]
                 + [functools.partial(norm_mid, g) for g in range(groups)])
 
@@ -323,24 +335,26 @@
             for which in range(2):
                 kv_copy(half, idx, which, core).wait_send()
 
-    late = jnp.where(core == 0, (chip == 3) | (chip >= 5), (chip == 0) | ((chip >= 4) & (chip <= 6))).astype(jnp.int32)
+    late = jnp.where(core == 0, (chip == 0) | ((chip >= 4) & (chip <= 6)), (chip == 3) | (chip >= 5)).astype(jnp.int32)
 
     def part_idx(part):
         return jnp.where(part == 1, late, 1 - late)
 
-    def tile_steps(half, part, buf, start, size, first):
+    def tile_steps(half, part, buf, start, size, first, only=None):
         rows = rows_of(part_idx(part) * q_len + start, size)
         where = pl.ds(0, size)
-        there = pl.ds(start, size)
+        there = rows_of(start, size)
 
         def up(sub):
-            cols = pl.ds(sub * F_SUB, F_SUB)
+            cols = rows_of(sub * F_SUB, F_SUB)
             hb[where, cols] = gelu_times(dot(mb[rows, :], w_g[buf, :, cols]), dot(mb[rows, :], w_u[buf, :, cols]))
 
         def down(cols):
             product = dot(hb[where, :], w_d[buf, :, cols])
             acc[part, there, cols] = product if first else acc[part, there, cols] + product
 
+        if only is not None:
+            return [functools.partial(up, only)]
         return ([functools.partial(up, sub) for sub in range(F_TILE // F_SUB)]
                 + [functools.partial(down, pl.ds(0, dim // 512 * 256)), functools.partial(down, pl.ds(dim // 512 * 256, dim - dim // 512 * 256))])
 
@@ -357,12 +371,13 @@
         post_ffw = scales[layer * 4 + 3]
 
         def norm_out(first_row):
-            for step in range(first_row, first_row + min(GROUP, size), 16):
+            for offset in range(0, GROUP, 16):
+                step = first_row + offset
                 those = rows_of(part_idx(part) * q_len + step, 16)
-                down = acc[part, pl.ds(step, 16), :].astype(BF16).astype(F32)
+                down = acc[part, rows_of(step, 16), :].astype(BF16).astype(F32)
                 xb[half, those, :] = (xb[half, those, :].astype(F32) + rms(down, post_ffw).astype(F32)).astype(BF16)
 
-        return [functools.partial(norm_out, row) for row in range(start, start + size, GROUP)]
+        return [functools.partial(norm_out, start + row) for row in range(0, size, GROUP)]
 
     def send_out(half, part, pieces):
         idx = part_idx(part)
@@ -383,7 +398,8 @@
     send_keys(0)
     run_all(steps_own(0, 0))
     await_keys(0)
-    run_all(steps_rest(0, 0))
+    lax.fori_loop(0, n_heads, lambda head, inner: (run_all(steps_rest(0, 0, head)), inner)[1], 0)
+    run_all(steps_rest(0, 0, heads=False))
     mb[...] = ab[...]
     await_sent_keys(0)
     last_stage = 3
@@ -418,7 +434,31 @@
 
             return inner
 
-        lax.fori_loop(0, jnp.where(count == last_stage, 6, 3), plain_tile, 0)
+        lax.fori_loop(0, jnp.where(count == last_stage, 5, 3), plain_tile, 0)
+
+        @pl.when(count == last_stage)
+        def _():
+            await_tile(buf_of(2))
+            ahead_of_me = lax.rem(2 * quarter_of(core, late) - chip + n_chips, n_chips)
+            last_half = jnp.where(ahead_of_me >= n_chips // 2, 1, 0)
+
+            def last_rows(turn, inner):
+                piece_half = jnp.where(turn == 1, last_half, 1 - last_half)
+                start = piece_half * (q_len // 2)
+
+                def up_steps(third, inner2):
+                    for sub in range(3):
+                        tile_steps(half, 1, buf_of(2), start, q_len // 2, False, third * 3 + sub)[0]()
+                    return inner2
+
+                lax.fori_loop(0, F_TILE // F_SUB // 3, up_steps, 0)
+                run_all(tile_steps(half, 1, buf_of(2), start, q_len // 2, False)[-2:])
+                run_all(out_steps(layer, half, 1, start, q_len // 2))
+                send_out(half, 1, [piece_half * (quarter // 2) + j for j in range(quarter // 2)])
+                return inner
+
+            lax.fori_loop(0, 2, last_rows, 0)
+
 
         @pl.when(count < last_stage)
         def _():
@@ -497,7 +537,6 @@
         scales = weights[7:11] + weights[18:22]
         matrices = weights[0:7] + weights[11:18]
         hbm = pl.BlockSpec(memory_space=pltpu.HBM)
-        vmem = pl.BlockSpec(memory_space=pltpu.VMEM)
         scratch = [
             pltpu.VMEM((2, n_tok, dim), BF16),
             pltpu.VMEM((n_tok, dim), BF16),
@@ -533,11 +572,14 @@
             pltpu.SemaphoreType.DMA((2, 2, 2)),
             pltpu.SemaphoreType.DMA((2, n_chips)),
             pltpu.SemaphoreType.DMA((2, n_chips)),
-        ]
+            pltpu.VMEM(positions.shape, jnp.int32),
+            pltpu.VMEM((1, HALF_DIM), F32),
+            pltpu.SemaphoreType.DMA((10,)),
+        ] + [pltpu.VMEM((dim,), F32)] * 8
         return pl.pallas_call(
             functools.partial(fused_kernel, cp_size),
             out_shape=jax.ShapeDtypeStruct(hidden.shape, BF16),
-            in_specs=[hbm] + [vmem] * 10 + [hbm] * 14,
+            in_specs=[hbm] * 25,
             out_specs=hbm,
             scratch_shapes=scratch,
             compiler_params=pltpu.CompilerParams(collective_id=0, has_side_effects=True, vmem_limit_bytes=67043328),

time: 209 us -> 208 us (level)
  no operation moved by 1% of the time
where the time goes in v4:
time: 208 us
  Pallas kernels  204 us (98%)
  local copies, waits for them, and re-layouts  3.26 us (2%)
    pallas_call x1, Pallas kernels, device_step(): pl.pallas_call(functools.partial(fused_kernel, cp_size), out_shape=jax.Sh...  204 us

profile of v4, /device:TPU:21, one launch (start us, length us, event | category | flops | bytes accessed | tf_op | source)
XLA Modules:
  0.0 207.6 jit_solution(16261347380756799177)
XLA Ops:
  0.0 204.4 %two_layers.1 = bf16[16,64,1152]{2,1,0:T(8,128)(2,1)} custom-call(bf16[16,64,1152]{2,1,0:T(8,128)(2,1)} %hidden.1, s32[16,64]{1,0:T(8,128)} %positions.1, f32[1,128]{1,0:T(1,128)} %constant.2.clone.inv_freq_in, f32[1152]{0:T(1024)} %refs_0_.1, f32[1152]{0:T(1024)} %refs_1_.1, f32[1152]{0:T(1024)} %refs_2_.1, f32[1152]{0:T(1024)} %refs_3_.1, f32[1152]{0:T(1024)} %refs_4_.1, ...), custom_call_target="tpu_custom_call" | custom-call | tf_op jit(solution)/shard_map/two_layers/pallas_call | solution.py:579
  204.4 3.3 %copy.27 = bf16[16,64,1152]{2,1,0:T(8,128)(2,1)} copy(bf16[16,64,1152]{2,1,0:T(8,128)(2,1)} %two_layers.1) | data formatting | bytes 4718592
